TPU v7x, 512 devices: a whole 4x8x8 slice. The times are simulated.
512 devices in a mesh: hyd: 8 (over y), tm: 16 (over z_hi, x), freq: 4 (over z_lo, core).
Axes of the slice: x: 4, y: 8, z: 8 (z_hi: 4, z_lo: 2; z = z_hi * 2 + z_lo), core: 2. Of those that a mesh axis runs over, the one named last changes fastest.
Arguments:
- spectra: bfloat16 [2, 16, 1024, 2048], P(None, 'tm', 'freq', 'hyd'), may hold values from -6 to 6
- row_lags: int32 [32, 512], replicated, may hold values from 0 to 31
- col_lags: int32 [64, 512], replicated, may hold values from 0 to 31
- replica: bfloat16 [2, 8192], replicated, may hold values from -0.0625 to 0.0625
- rep_len: int32 [1], replicated, may hold values from 4096 to 8192
Outputs:
- echoes: float32 [512, 2, 16384], P(('hyd', 'freq'), None, 'tm')
All inputs are finite; a program needn't handle non-finite values.
Results may differ from a plain program's by a relative error of at most 0.011.
Values may be sent and summed in bfloat16 or wider, within the bound.
A program may use at most 64 MiB of HBM per device.

v0:
```python
import math

import jax
import jax.numpy as jnp
from jax import lax
from jax.sharding import PartitionSpec as P

ARRAY_ROWS = 32
ARRAY_COLS = 64
BINS = 1024
REPLICA = 8192
BLOCK = 256


two_pi = 2.0 * math.pi
group_count = 4


def split_up(shard, dim, count):
    before, after = (shard.shape[:dim], shard.shape[dim + 1 :])
    return jnp.moveaxis(shard.reshape(*before, count, -1, *after), dim, 0)


def sum_at_owner(shard, axis, dim):
    blocks = split_up(shard, dim, lax.axis_size(axis))
    arrived = lax.all_to_all(blocks, axis, split_axis=0, concat_axis=0, tiled=True)
    return arrived.sum(axis=0)


def from_behind(value, axis, steps):
    count = lax.axis_size(axis)
    initial, last = (max(0, -steps), min(count, count - steps))
    return lax.ppermute(value, axis, [(source, source + steps) for source in range(initial, last)])


def steering(bin_index, lag_table, factor):
    period = 2 * BINS
    phase = bin_index[:, None, None] * lag_table[None] % period
    angles = phase.astype(jnp.float32) * (two_pi / period)
    return (
        (jnp.cos(angles) * factor).astype(jnp.bfloat16),
        (jnp.sin(angles) * factor).astype(jnp.bfloat16),
    )


def beamform(spectra, row_lags, col_lags, bin_index):
    frame_count = spectra.shape[1]
    local_bins = spectra.shape[2]
    row_count = row_lags.shape[0]
    col_count = col_lags.shape[0]
    beam_count = col_lags.shape[1]
    bin_width = math.gcd(local_bins, max(1, min(16, 512 // (2 * frame_count * row_count))))
    bin_blocks = local_bins // bin_width
    arranged = spectra.reshape(2, frame_count, bin_blocks, bin_width, row_count, col_count)
    arranged = jnp.transpose(arranged, (2, 3, 0, 1, 4, 5)).reshape(
        bin_blocks, bin_width, 2 * frame_count * row_count, col_count
    )
    chosen_bins = bin_index.reshape(bin_blocks, bin_width)

    def one_block(pair_in):
        slab_in, block_bins = pair_in
        col_re, col_im = steering(block_bins, col_lags, ARRAY_COLS ** (-0.5))
        weights = jnp.concatenate([col_re, col_im], axis=2)
        products = jnp.einsum("fmc,fcn->fmn", slab_in, weights, preferred_element_type=jnp.float32)
        products = products.reshape(bin_width, 2, frame_count * row_count, 2 * beam_count)
        along_re = products[:, 0, :, :beam_count] - products[:, 1, :, beam_count:]
        along_im = products[:, 0, :, beam_count:] + products[:, 1, :, :beam_count]
        along_re = along_re.reshape(bin_width, frame_count, row_count, beam_count)
        along_im = along_im.reshape(bin_width, frame_count, row_count, beam_count)
        row_re, row_im = steering(block_bins, row_lags, ARRAY_ROWS ** (-0.5))
        row_re = row_re.astype(jnp.float32)[:, None]
        row_im = row_im.astype(jnp.float32)[:, None]
        beam_re = jnp.sum(along_re * row_re - along_im * row_im, axis=2)
        beam_im = jnp.sum(along_re * row_im + along_im * row_re, axis=2)
        return jnp.stack([beam_re, beam_im], axis=2)

    formed = lax.map(one_block, (arranged, chosen_bins))
    return formed.reshape(local_bins, frame_count, 2, beam_count)


def transform_tables(first_bin, bin_total):
    freqs = first_bin + jnp.arange(bin_total, dtype=jnp.int32)
    samples = jnp.arange(BINS, dtype=jnp.int32)
    phase = freqs[:, None] * samples[None] % BINS
    angles = phase.astype(jnp.float32) * (two_pi / BINS)
    factor = BINS ** (-0.5)
    return (
        (jnp.cos(angles) * factor).astype(jnp.bfloat16),
        (jnp.sin(angles) * factor).astype(jnp.bfloat16),
    )


def inverse(spectra_b, tab_re, tab_im):
    lead_beams = spectra_b.shape[0]
    lead_frames = spectra_b.shape[1]
    bin_total = spectra_b.shape[3]
    beam_total = lead_beams * lead_frames
    part_re = spectra_b[:, :, 0].reshape(beam_total, bin_total)
    part_im = spectra_b[:, :, 1].reshape(beam_total, bin_total)
    out_re = jnp.dot(part_re, tab_re, preferred_element_type=jnp.float32) - jnp.dot(
        part_im, tab_im, preferred_element_type=jnp.float32
    )
    out_im = jnp.dot(part_re, tab_im, preferred_element_type=jnp.float32) + jnp.dot(
        part_im, tab_re, preferred_element_type=jnp.float32
    )
    return jnp.stack([out_re, out_im], axis=1).reshape(lead_beams, lead_frames * 2 * BINS)


def on_device(spectra, row_lags, col_lags, replica, rep_len):
    local_bins = spectra.shape[2]
    freq_index = lax.axis_index("freq")
    hyd_index = lax.axis_index("hyd")
    band_first = BINS // 2 + freq_index * local_bins
    moved = lax.all_to_all(spectra, "hyd", split_axis=2, concat_axis=3, tiled=True)
    bins_part = moved.shape[2]
    bin_index = band_first + hyd_index * bins_part + jnp.arange(bins_part, dtype=jnp.int32)
    formed = beamform(moved, row_lags, col_lags, bin_index).astype(jnp.bfloat16)
    returned = lax.all_to_all(formed, "hyd", split_axis=3, concat_axis=0, tiled=True)
    owned = jnp.transpose(returned, (3, 1, 2, 0))
    frame_count = owned.shape[1]
    tab_re, tab_im = transform_tables(freq_index * local_bins, local_bins)
    series = sum_at_owner(inverse(owned, tab_re, tab_im), "freq", 0)
    series = series.astype(jnp.bfloat16)
    beam_local = series.shape[0]
    span = frame_count * BINS
    own_series = jnp.transpose(
        series.reshape(beam_local, frame_count, 2, BINS), (2, 0, 1, 3)
    ).reshape(2, beam_local, span)
    block_count = span // BLOCK
    rim_count = REPLICA // span
    rim_list = []
    carried = own_series
    for hop_count in range(rim_count):
        carried = from_behind(carried, "tm", -1)
        rim_list.append(carried)
    tap_count = REPLICA // BLOCK + 1
    padded = -(-tap_count // group_count) * group_count
    groups = padded // group_count
    window = padded * BLOCK
    filler = jnp.zeros((2, beam_local, window - BLOCK - REPLICA), jnp.bfloat16)
    extended = jnp.concatenate([own_series] + rim_list + [filler], axis=2)
    kept_mask = jnp.arange(REPLICA, dtype=jnp.int32) < rep_len[0]
    masked = jnp.where(kept_mask[None], replica, jnp.zeros_like(replica))
    padded_pulse = jnp.concatenate(
        [
            jnp.zeros((2, BLOCK), jnp.bfloat16),
            masked,
            jnp.zeros((2, window + 1 - REPLICA), jnp.bfloat16),
        ],
        axis=1,
    )
    pulse_span = padded_pulse.shape[1]
    tiled = jnp.tile(padded_pulse, (1, BLOCK))[:, : BLOCK * (pulse_span - 1)]
    toeplitz = tiled.reshape(2, BLOCK, pulse_span - 1)[:, :, BLOCK : BLOCK + window].reshape(
        2 * BLOCK, window
    )
    row_total = 2 * beam_local * block_count

    def group_step(group_index, running):
        first_col = group_index * (group_count * BLOCK)
        hankel_parts = []
        for member in range(group_count):
            slab = lax.dynamic_slice_in_dim(extended, first_col + member * BLOCK, span, 2)
            hankel_parts.append(slab.reshape(row_total, BLOCK))
        stacked = jnp.concatenate(hankel_parts, axis=1)
        weights = lax.dynamic_slice_in_dim(toeplitz, first_col, group_count * BLOCK, 1)
        product = lax.dot_general(
            stacked, weights, (((1,), (1,)), ((), ())), preferred_element_type=jnp.float32
        )
        return running + product

    running = lax.fori_loop(0, groups, group_step, jnp.zeros((row_total, 2 * BLOCK), jnp.float32))
    result = running.reshape(2, beam_local, block_count, 2, BLOCK)
    echo_re = result[0, :, :, 0] + result[1, :, :, 1]
    echo_im = result[1, :, :, 0] - result[0, :, :, 1]
    return jnp.stack([echo_re.reshape(beam_local, span), echo_im.reshape(beam_local, span)], axis=1)


def solution(mesh):
    placed = (P(None, "tm", "freq", "hyd"), P(), P(), P(), P())
    return jax.shard_map(
        on_device,
        mesh=mesh,
        in_specs=placed,
        out_specs=P(("hyd", "freq"), None, "tm"),
        check_vma=False,
    )
```

profile of v0, /device:TPU:198, one launch (start us, length us, event | category | flops | bytes accessed | tf_op | source)
XLA Modules:
  0.0 271.7 jit_solution(7165303118007343716)
XLA Ops:
  0.0 1.9 copy.79
  1.9 7.1 %all-to-all-start = ((bf16[2,1,256,256]{3,0,1,2:T(2,128)(2,1)}), bf16[2,1,256,256]{3,0,1,2:T(2,128)(2,1)S(1)}, u32[]{:S(2)}, u32[]{:S(2)}) async-start(bf16[2,1,256,256]{3,0,1,2:T(2,128)(2,1)} %copy.79), calls=%async_computation | async-start | bytes 524288 | tf_op jit(solution)/shard_map/all_to_all | solution.py:114
  9.7 11.2 %all-to-all-done = bf16[2,1,256,256]{3,0,1,2:T(2,128)(2,1)S(1)} async-done(((bf16[2,1,256,256]{3,0,1,2:T(2,128)(2,1)}), bf16[2,1,256,256]{3,0,1,2:T(2,128)(2,1)S(1)}, u32[]{:S(2)}, u32[]{:S(2)}) %all-to-all-start) | async-done | bytes 262176 | tf_op jit(solution)/shard_map/all_to_all | solution.py:114
  21.1 0.2 reshape.218
  21.4 38.3 %while.28 = (s32[]{:T(128)}, bf16[4,8,1,2,512]{4,1,0,3,2:T(8,128)(2,1)S(1)}, bf16[4,8,64,64]{3,2,1,0:T(8,128)(2,1)S(1)}, s32[4,8]{1,0:T(4,128)S(1)}, s32[64,512]{1,0:T(8,128)}, /*index=5*/s32[32,512]{1,0:T(8,128)}, s32[]{:T(128)}) while((s32[]{:T(128)}, bf16[4,8,1,2,512]{4,1,0,3,2:T(8,128)(2,1)S(1)}, bf16[4,8,64,64]{3,2,1,0:T(8,128)(2,1)S(1)}, ...), condition=%wide.region_3.4_spmd, body=%wide.region_0.3_spmd.sunk | while | flops 77881344 | bytes 6734041 | solution.py:77
  21.4 5.5 %multiply_convert_fusion.11 = (bf16[8,64,512]{2,1,0:T(8,128)(2,1)S(1)}, bf16[8,64,512]{2,1,0:T(8,128)(2,1)S(1)}) fusion(s32[64,512]{1,0:T(8,128)} %get-tuple-element.366, s32[8]{0:T(128)S(1)} %fusion.69), kind=kLoop, calls=%fused_computation.13.clone.1 | loop fusion | flops 4718592 | bytes 1179680 | tf_op jit(solution)/shard_map/while/body/eval_jaxpr/convert_element_type | solution.py:41
  26.9 0.4 fusion.70
  27.3 3.5 %fusion.71 = (bf16[8,512]{1,0:T(8,128)(2,1)S(1)}, bf16[8,512]{1,0:T(8,128)(2,1)S(1)}) fusion(s32[32,512]{1,0:T(8,128)} %get-tuple-element.367, s32[8]{0:T(128)S(1)} %fusion.69, f32[8,2,32,1024]{3,2,1,0:T(8,128)S(1)} %bitcast.68), kind=kLoop, calls=%fused_computation.24.clone.1 | loop fusion | flops 3923968 | bytes 2179104 | tf_op jit(solution)/shard_map/while/body/eval_jaxpr/reduce_sum | solution.py:73
  31.0 5.5 %multiply_convert_fusion.11 = (bf16[8,64,512]{2,1,0:T(8,128)(2,1)S(1)}, bf16[8,64,512]{2,1,0:T(8,128)(2,1)S(1)}) fusion(s32[64,512]{1,0:T(8,128)} %get-tuple-element.366, s32[8]{0:T(128)S(1)} %fusion.69), kind=kLoop, calls=%fused_computation.13.clone.1 | loop fusion | flops 4718592 | bytes 1179680 | tf_op jit(solution)/shard_map/while/body/eval_jaxpr/convert_element_type | solution.py:41
  36.5 0.4 fusion.70
  36.9 3.5 %fusion.71 = (bf16[8,512]{1,0:T(8,128)(2,1)S(1)}, bf16[8,512]{1,0:T(8,128)(2,1)S(1)}) fusion(s32[32,512]{1,0:T(8,128)} %get-tuple-element.367, s32[8]{0:T(128)S(1)} %fusion.69, f32[8,2,32,1024]{3,2,1,0:T(8,128)S(1)} %bitcast.68), kind=kLoop, calls=%fused_computation.24.clone.1 | loop fusion | flops 3923968 | bytes 2179104 | tf_op jit(solution)/shard_map/while/body/eval_jaxpr/reduce_sum | solution.py:73
  40.6 5.5 %multiply_convert_fusion.11 = (bf16[8,64,512]{2,1,0:T(8,128)(2,1)S(1)}, bf16[8,64,512]{2,1,0:T(8,128)(2,1)S(1)}) fusion(s32[64,512]{1,0:T(8,128)} %get-tuple-element.366, s32[8]{0:T(128)S(1)} %fusion.69), kind=kLoop, calls=%fused_computation.13.clone.1 | loop fusion | flops 4718592 | bytes 1179680 | tf_op jit(solution)/shard_map/while/body/eval_jaxpr/convert_element_type | solution.py:41
  46.1 0.4 fusion.70
  46.5 3.5 %fusion.71 = (bf16[8,512]{1,0:T(8,128)(2,1)S(1)}, bf16[8,512]{1,0:T(8,128)(2,1)S(1)}) fusion(s32[32,512]{1,0:T(8,128)} %get-tuple-element.367, s32[8]{0:T(128)S(1)} %fusion.69, f32[8,2,32,1024]{3,2,1,0:T(8,128)S(1)} %bitcast.68), kind=kLoop, calls=%fused_computation.24.clone.1 | loop fusion | flops 3923968 | bytes 2179104 | tf_op jit(solution)/shard_map/while/body/eval_jaxpr/reduce_sum | solution.py:73
  50.2 5.5 %multiply_convert_fusion.11 = (bf16[8,64,512]{2,1,0:T(8,128)(2,1)S(1)}, bf16[8,64,512]{2,1,0:T(8,128)(2,1)S(1)}) fusion(s32[64,512]{1,0:T(8,128)} %get-tuple-element.366, s32[8]{0:T(128)S(1)} %fusion.69), kind=kLoop, calls=%fused_computation.13.clone.1 | loop fusion | flops 4718592 | bytes 1179680 | tf_op jit(solution)/shard_map/while/body/eval_jaxpr/convert_element_type | solution.py:41
  55.6 0.4 fusion.70
  56.1 3.5 %fusion.71 = (bf16[8,512]{1,0:T(8,128)(2,1)S(1)}, bf16[8,512]{1,0:T(8,128)(2,1)S(1)}) fusion(s32[32,512]{1,0:T(8,128)} %get-tuple-element.367, s32[8]{0:T(128)S(1)} %fusion.69, f32[8,2,32,1024]{3,2,1,0:T(8,128)S(1)} %bitcast.68), kind=kLoop, calls=%fused_computation.24.clone.1 | loop fusion | flops 3923968 | bytes 2179104 | tf_op jit(solution)/shard_map/while/body/eval_jaxpr/reduce_sum | solution.py:73
  59.9 0.9 reshape.230
  60.8 3.6 %all-to-all-start.1 = ((bf16[8,2,2048]{2,1,0:T(2,128)(2,1)}), bf16[8,2,2048]{2,1,0:T(2,128)(2,1)S(1)}, u32[]{:S(2)}, u32[]{:S(2)}) async-start(bf16[8,2,2048]{2,1,0:T(2,128)(2,1)} %reshape.230), calls=%async_computation.1 | async-start | bytes 131072 | tf_op jit(solution)/shard_map/all_to_all | solution.py:118
  64.5 7.9 %all-to-all-done.1 = bf16[8,2,2048]{2,1,0:T(2,128)(2,1)S(1)} async-done(((bf16[8,2,2048]{2,1,0:T(2,128)(2,1)}), bf16[8,2,2048]{2,1,0:T(2,128)(2,1)S(1)}, u32[]{:S(2)}, u32[]{:S(2)}) %all-to-all-start.1) | async-done | bytes 65568 | tf_op jit(solution)/shard_map/all_to_all | solution.py:118
  72.5 0.2 reshape.231
  72.7 0.2 copy.97
  72.8 4.0 %fusion.37 = f32[64,1024]{1,0:T(8,128)S(1)} fusion(s32[256]{0:T(256)S(1)} %iota_add_fusion, bf16[64,1,2,256]{0,3,2,1:T(8,128)(2,1)S(1)} %bitcast.78), kind=kOutput, calls=%fused_computation.74 | convolution fusion | flops 37748736 | bytes 328704 | tf_op jit(solution)/shard_map/dot_general | solution.py:100
  76.9 4.1 %fusion.38 = f32[64,1024]{1,0:T(8,128)S(1)} fusion(s32[256]{0:T(256)S(1)} %iota_add_fusion, bf16[64,1,2,256]{0,3,2,1:T(8,128)(2,1)S(1)} %bitcast.79), kind=kOutput, calls=%fused_computation.75 | convolution fusion | flops 37748736 | bytes 328704 | tf_op jit(solution)/shard_map/dot_general | solution.py:103
  81.0 4.5 %fusion.30 = f32[64,1,1024]{2,0,1:T(8,128)S(1)} fusion(f32[64,1024]{1,0:T(8,128)S(1)} %fusion.37, s32[256]{0:T(256)S(1)} %iota_add_fusion, bf16[64,1,2,256]{0,3,2,1:T(8,128)(2,1)S(1)} %bitcast.80), kind=kOutput, calls=%fused_computation.64 | convolution fusion | flops 37814272 | bytes 590848 | tf_op jit(solution)/shard_map/dot_general | solution.py:100
  85.5 4.1 %fusion.29 = f32[64,1,1024]{2,0,1:T(8,128)S(1)} fusion(f32[64,1024]{1,0:T(8,128)S(1)} %fusion.38, s32[256]{0:T(256)S(1)} %iota_add_fusion, bf16[64,1,2,256]{0,3,2,1:T(8,128)(2,1)S(1)} %bitcast.81), kind=kOutput, calls=%fused_computation.62 | convolution fusion | flops 37814272 | bytes 590848 | tf_op jit(solution)/shard_map/dot_general | solution.py:103
  89.6 0.4 copy.89
  90.0 1.2 reshape_reshape.3
  91.3 3.5 %all-to-all-start.2 = ((f32[4,16,2048]{2,1,0:T(8,128)}), f32[4,16,2048]{2,1,0:T(8,128)S(1)}, u32[]{:S(2)}, u32[]{:S(2)}) async-start(f32[4,16,2048]{2,1,0:T(8,128)} %reshape_reshape.3), calls=%async_computation.2 | async-start | bytes 1048576 | tf_op jit(solution)/shard_map/all_to_all | solution.py:26
  94.8 4.4 %tile.4 = bf16[2,256,9473]{2,1,0:T(8,128)(2,1)} broadcast(bf16[2,9473]{1,0:T(2,128)(2,1)S(1)} %maximum_maximum_fusion), dimensions={0,2} | broadcast | bytes 9738244 | tf_op jit(solution)/shard_map/tile | solution.py:153
  99.2 24.3 %reshape.228 = bf16[4850176]{0:T(1024)(128)(2,1)} reshape(bf16[2,256,9473]{2,1,0:T(8,128)(2,1)} %tile.4) | data formatting | bytes 19400704
  123.6 17.8 %tile.10 = bf16[2,2425088]{1,0:T(2,128)(2,1)} reshape(bf16[4850176]{0:T(1024)(128)(2,1)} %reshape.228) | data formatting | bytes 19400704 | tf_op jit(solution)/shard_map/tile | solution.py:153
  141.3 9.3 %slice.62 = bf16[2,2424832]{1,0:T(2,128)(2,1)} slice(bf16[2,2425088]{1,0:T(2,128)(2,1)} %tile.10), slice={[0:2], [0:2424832]} | slice | bytes 19398656 | tf_op jit(solution)/shard_map/slice | solution.py:153
  150.7 8.4 %copy.112 = bf16[1,2,256,9472]{3,2,1,0:T(8,128)(2,1)} copy(bf16[1,2,256,9472]{3,1,2,0:T(2,128)(2,1)} %bitcast.69) | data formatting | bytes 19398656
  159.1 7.9 %slice.63 = bf16[2,256,9216]{2,1,0:T(8,128)(2,1)} slice(bf16[2,256,9472]{2,1,0:T(8,128)(2,1)} %bitcast.70), slice={[0:2], [0:256], [256:9472]} | slice | bytes 18874368 | tf_op jit(solution)/shard_map/slice | solution.py:154
  167.1 2.7 %collective-permute-start = (bf16[2,16,1024]{2,0,1:T(2,128)(2,1)S(1)}, bf16[2,16,1024]{2,0,1:T(2,128)(2,1)S(1)}, u32[]{:S(2)}, u32[]{:S(2)}) collective-permute-start(bf16[2,16,1024]{2,0,1:T(2,128)(2,1)S(1)} %bitcast.77), channel_id=1, source_target_pairs={{4,0},{8,4},{12,8},{16,12},{20,16},{24,20},{28,24},{32,28},{36,32}... | collective-permute-start | bytes 196616 | tf_op jit(solution)/shard_map/ppermute | solution.py:33
  169.9 7.6 %collective-permute-done = bf16[2,16,1024]{2,0,1:T(2,128)(2,1)S(1)} collective-permute-done((bf16[2,16,1024]{2,0,1:T(2,128)(2,1)S(1)}, bf16[2,16,1024]{2,0,1:T(2,128)(2,1)S(1)}, u32[]{:S(2)}, u32[]{:S(2)}) %collective-permute-start) | collective-permute-done | bytes 65568 | tf_op jit(solution)/shard_map/ppermute | solution.py:33
  177.4 1.9 collective-permute-start.1
  179.4 8.5 %collective-permute-done.1 = bf16[2,16,1024]{2,0,1:T(2,128)(2,1)S(1)} collective-permute-done((bf16[2,16,1024]{2,0,1:T(2,128)(2,1)S(1)}, bf16[2,16,1024]{2,0,1:T(2,128)(2,1)S(1)}, u32[]{:S(2)}, u32[]{:S(2)}) %collective-permute-start.1) | collective-permute-done | bytes 65568 | tf_op jit(solution)/shard_map/ppermute | solution.py:33
  188.0 1.9 collective-permute-start.2
  189.9 8.4 %collective-permute-done.2 = bf16[2,16,1024]{2,0,1:T(2,128)(2,1)S(1)} collective-permute-done((bf16[2,16,1024]{2,0,1:T(2,128)(2,1)S(1)}, bf16[2,16,1024]{2,0,1:T(2,128)(2,1)S(1)}, u32[]{:S(2)}, u32[]{:S(2)}) %collective-permute-start.2) | collective-permute-done | bytes 65568 | tf_op jit(solution)/shard_map/ppermute | solution.py:33
  198.3 1.9 collective-permute-start.3
  200.3 9.1 %collective-permute-done.3 = bf16[2,16,1024]{2,0,1:T(2,128)(2,1)S(1)} collective-permute-done((bf16[2,16,1024]{2,0,1:T(2,128)(2,1)S(1)}, bf16[2,16,1024]{2,0,1:T(2,128)(2,1)S(1)}, u32[]{:S(2)}, u32[]{:S(2)}) %collective-permute-start.3) | collective-permute-done | bytes 65568 | tf_op jit(solution)/shard_map/ppermute | solution.py:33
  209.4 1.9 collective-permute-start.4
  211.4 8.8 %collective-permute-done.4 = bf16[2,16,1024]{2,0,1:T(2,128)(2,1)S(1)} collective-permute-done((bf16[2,16,1024]{2,0,1:T(2,128)(2,1)S(1)}, bf16[2,16,1024]{2,0,1:T(2,128)(2,1)S(1)}, u32[]{:S(2)}, u32[]{:S(2)}) %collective-permute-start.4) | collective-permute-done | bytes 65568 | tf_op jit(solution)/shard_map/ppermute | solution.py:33
  220.1 1.9 collective-permute-start.5
  222.1 8.4 %collective-permute-done.5 = bf16[2,16,1024]{2,0,1:T(2,128)(2,1)S(1)} collective-permute-done((bf16[2,16,1024]{2,0,1:T(2,128)(2,1)S(1)}, bf16[2,16,1024]{2,0,1:T(2,128)(2,1)S(1)}, u32[]{:S(2)}, u32[]{:S(2)}) %collective-permute-start.5) | collective-permute-done | bytes 65568 | tf_op jit(solution)/shard_map/ppermute | solution.py:33
  230.5 1.9 collective-permute-start.6
  232.5 8.5 %collective-permute-done.6 = bf16[2,16,1024]{2,0,1:T(2,128)(2,1)S(1)} collective-permute-done((bf16[2,16,1024]{2,0,1:T(2,128)(2,1)S(1)}, bf16[2,16,1024]{2,0,1:T(2,128)(2,1)S(1)}, u32[]{:S(2)}, u32[]{:S(2)}) %collective-permute-start.6) | collective-permute-done | bytes 65568 | tf_op jit(solution)/shard_map/ppermute | solution.py:33
  241.0 1.9 collective-permute-start.7
  242.9 8.4 %collective-permute-done.7 = bf16[2,16,1024]{2,0,1:T(2,128)(2,1)S(1)} collective-permute-done((bf16[2,16,1024]{2,0,1:T(2,128)(2,1)S(1)}, bf16[2,16,1024]{2,0,1:T(2,128)(2,1)S(1)}, u32[]{:S(2)}, u32[]{:S(2)}) %collective-permute-start.7) | collective-permute-done | bytes 65568 | tf_op jit(solution)/shard_map/ppermute | solution.py:33
  251.5 18.6 %while.29 = (s32[]{:T(128)}, f32[128,512]{1,0:T(8,128)S(1)}, bf16[2,16,9984]{2,1,0:T(8,128)(2,1)S(1)}, bf16[512,9216]{1,0:T(8,128)(2,1)}, s32[]{:T(128)}, /*inde...) while((s32[]{:T(128)}, f32[128,512]{1,0:T(8,128)S(1)}, ...), condition=%wide.region_6.7_spmd.clone, body=%wide.region_5.6_spmd.clone.sunk | while | flops 135397392 | bytes 2883964 | solution.py:172
  251.8 1.7 convolution_add_fusion.3
  253.9 1.7 convolution_add_fusion.3
  256.0 1.7 convolution_add_fusion.3
  258.0 1.7 convolution_add_fusion.3
  260.1 1.7 convolution_add_fusion.3
  262.2 1.7 convolution_add_fusion.3
  264.2 1.7 convolution_add_fusion.3
  266.3 1.7 convolution_add_fusion.3
  268.4 1.7 convolution_add_fusion.3
  270.1 0.2 reshape.223
  270.3 0.2 fusion.59
  270.7 0.8 copy.95
  (101 shorter events, 3.9 us)
Async XLA Ops:
  1.9 19.0 %all-to-all-start = ((bf16[2,1,256,256]{3,0,1,2:T(2,128)(2,1)}), bf16[2,1,256,256]{3,0,1,2:T(2,128)(2,1)S(1)}, u32[]{:S(2)}, u32[]{:S(2)}) async-start(bf16[2,1,256,256]{3,0,1,2:T(2,128)(2,1)} %copy.79), calls=%async_computation | async-start | bytes 524288 | tf_op jit(solution)/shard_map/all_to_all | solution.py:114
  21.4 43.0 %copy-start = (bf16[2,8192]{1,0:T(2,128)(2,1)S(1)}, bf16[2,8192]{1,0:T(2,128)(2,1)}, u32[]{:S(2)}) copy-start(bf16[2,8192]{1,0:T(2,128)(2,1)} %param.12) | copy-start | bytes 98308
  60.8 11.7 %all-to-all-start.1 = ((bf16[8,2,2048]{2,1,0:T(2,128)(2,1)}), bf16[8,2,2048]{2,1,0:T(2,128)(2,1)S(1)}, u32[]{:S(2)}, u32[]{:S(2)}) async-start(bf16[8,2,2048]{2,1,0:T(2,128)(2,1)} %reshape.230), calls=%async_computation.1 | async-start | bytes 131072 | tf_op jit(solution)/shard_map/all_to_all | solution.py:118
  91.3 75.7 %all-to-all-start.2 = ((f32[4,16,2048]{2,1,0:T(8,128)}), f32[4,16,2048]{2,1,0:T(8,128)S(1)}, u32[]{:S(2)}, u32[]{:S(2)}) async-start(f32[4,16,2048]{2,1,0:T(8,128)} %reshape_reshape.3), calls=%async_computation.2 | async-start | bytes 1048576 | tf_op jit(solution)/shard_map/all_to_all | solution.py:26
  167.1 10.4 %collective-permute-start = (bf16[2,16,1024]{2,0,1:T(2,128)(2,1)S(1)}, bf16[2,16,1024]{2,0,1:T(2,128)(2,1)S(1)}, u32[]{:S(2)}, u32[]{:S(2)}) collective-permute-start(bf16[2,16,1024]{2,0,1:T(2,128)(2,1)S(1)} %bitcast.77), channel_id=1, source_target_pairs={{4,0},{8,4},{12,8},{16,12},{20,16},{24,20},{28,24},{32,28},{36,32}... | collective-permute-start | bytes 196616 | tf_op jit(solution)/shard_map/ppermute | solution.py:33
  177.4 10.5 %collective-permute-start.1 = (bf16[2,16,1024]{2,0,1:T(2,128)(2,1)S(1)}, bf16[2,16,1024]{2,0,1:T(2,128)(2,1)S(1)}, u32[]{:S(2)}, u32[]{:S(2)}) collective-permute-start(bf16[2,16,1024]{2,0,1:T(2,128)(2,1)S(1)} %collective-permute-done), channel_id=1, source_target_pairs={{4,0},{8,4},{12,8},{16,12},{20,16},{24,20},{28,24},{32,28},{36,32}... | collective-permute-start | bytes 196616 | tf_op jit(solution)/shard_map/ppermute | solution.py:33
  188.0 10.4 %collective-permute-start.2 = (bf16[2,16,1024]{2,0,1:T(2,128)(2,1)S(1)}, bf16[2,16,1024]{2,0,1:T(2,128)(2,1)S(1)}, u32[]{:S(2)}, u32[]{:S(2)}) collective-permute-start(bf16[2,16,1024]{2,0,1:T(2,128)(2,1)S(1)} %collective-permute-done.1), channel_id=1, source_target_pairs={{4,0},{8,4},{12,8},{16,12},{20,16},{24,20},{28,24},{32,28},{36,32}... | collective-permute-start | bytes 196616 | tf_op jit(solution)/shard_map/ppermute | solution.py:33
  198.3 11.1 %collective-permute-start.3 = (bf16[2,16,1024]{2,0,1:T(2,128)(2,1)S(1)}, bf16[2,16,1024]{2,0,1:T(2,128)(2,1)S(1)}, u32[]{:S(2)}, u32[]{:S(2)}) collective-permute-start(bf16[2,16,1024]{2,0,1:T(2,128)(2,1)S(1)} %collective-permute-done.2), channel_id=1, source_target_pairs={{4,0},{8,4},{12,8},{16,12},{20,16},{24,20},{28,24},{32,28},{36,32}... | collective-permute-start | bytes 196616 | tf_op jit(solution)/shard_map/ppermute | solution.py:33
  209.4 10.7 %collective-permute-start.4 = (bf16[2,16,1024]{2,0,1:T(2,128)(2,1)S(1)}, bf16[2,16,1024]{2,0,1:T(2,128)(2,1)S(1)}, u32[]{:S(2)}, u32[]{:S(2)}) collective-permute-start(bf16[2,16,1024]{2,0,1:T(2,128)(2,1)S(1)} %collective-permute-done.3), channel_id=1, source_target_pairs={{4,0},{8,4},{12,8},{16,12},{20,16},{24,20},{28,24},{32,28},{36,32}... | collective-permute-start | bytes 196616 | tf_op jit(solution)/shard_map/ppermute | solution.py:33
  220.1 10.4 %collective-permute-start.5 = (bf16[2,16,1024]{2,0,1:T(2,128)(2,1)S(1)}, bf16[2,16,1024]{2,0,1:T(2,128)(2,1)S(1)}, u32[]{:S(2)}, u32[]{:S(2)}) collective-permute-start(bf16[2,16,1024]{2,0,1:T(2,128)(2,1)S(1)} %collective-permute-done.4), channel_id=1, source_target_pairs={{4,0},{8,4},{12,8},{16,12},{20,16},{24,20},{28,24},{32,28},{36,32}... | collective-permute-start | bytes 196616 | tf_op jit(solution)/shard_map/ppermute | solution.py:33
  230.5 10.5 %collective-permute-start.6 = (bf16[2,16,1024]{2,0,1:T(2,128)(2,1)S(1)}, bf16[2,16,1024]{2,0,1:T(2,128)(2,1)S(1)}, u32[]{:S(2)}, u32[]{:S(2)}) collective-permute-start(bf16[2,16,1024]{2,0,1:T(2,128)(2,1)S(1)} %collective-permute-done.5), channel_id=1, source_target_pairs={{4,0},{8,4},{12,8},{16,12},{20,16},{24,20},{28,24},{32,28},{36,32}... | collective-permute-start | bytes 196616 | tf_op jit(solution)/shard_map/ppermute | solution.py:33
  241.0 10.4 %collective-permute-start.7 = (bf16[2,16,1024]{2,0,1:T(2,128)(2,1)S(1)}, bf16[2,16,1024]{2,0,1:T(2,128)(2,1)S(1)}, u32[]{:S(2)}, u32[]{:S(2)}) collective-permute-start(bf16[2,16,1024]{2,0,1:T(2,128)(2,1)S(1)} %collective-permute-done.6), channel_id=1, source_target_pairs={{4,0},{8,4},{12,8},{16,12},{20,16},{24,20},{28,24},{32,28},{36,32}... | collective-permute-start | bytes 196616 | tf_op jit(solution)/shard_map/ppermute | solution.py:33
where the time goes:
time: 276 us; the launch traced here: 272 us
  waiting for transfers between devices  86.7 us (31%)
  local copies, waits for them, and re-layouts  81.8 us (30%)
  other arithmetic  36.6 us (13%)
  matrix products  34 us (12%)
  starting transfers between devices  30.2 us (11%)
    ppermute x8, waiting for transfers between devices, from_behind(): lax.ppermute(value, axis, [(source, source + steps) for source in range(i...  67.6 us
    unnamed x17, local copies, waits for them, and re-layouts  36.3 us
    another operation x2, local copies, waits for them, and re-layouts, on_device(): tiled = jnp.tile(padded_pulse, (1, BLOCK))[:, :BLOCK * (pulse_span - 1)]  22.2 us
    convert_element_type x4, other arithmetic, steering(): (jnp.cos(angles) * factor).astype(jnp.bfloat16)  21.9 us
    ppermute x8, starting transfers between devices, from_behind(): lax.ppermute(value, axis, [(source, source + steps) for source in range(i...  16.1 us
    dot_general x9, matrix products, group_step(): lax.dot_general(stacked, weights, (((1,), (1,)), ((), ())), preferred_ele...  15.6 us
    reduce_sum x4, other arithmetic, one_block(): beam_re = jnp.sum(along_re * row_re - along_im * row_im, axis=2)  14.2 us
    all_to_all x1, waiting for transfers between devices, on_device(): lax.all_to_all(spectra, 'hyd', split_axis=2, concat_axis=3, tiled=True)  11.2 us
  transfers between devices with their start and end apart: 11, of which 10 were waited for; matrix products, arithmetic and copies ran while one was open for 27% of the time, Pallas kernels for 0%

commit v1 on v0

v1 whole, which is shorter than its diff:
```python
import math

import jax
import jax.numpy as jnp
import numpy as np
from jax import lax
from jax.experimental import pallas as pl
from jax.experimental.pallas import tpu as pltpu
from jax.sharding import PartitionSpec as P

ROWS = 32
COLS = 64
BINS = 1024
BEAMS = 512
FRAMES = 16
REPLICA = 8192
PERIOD = 2 * BINS
LOCAL_BINS = 32
TAPS = REPLICA // 128 + 1


def start_powers():
    table = np.zeros((32, 16), np.float64)
    for place in range(32):
        first = BINS // 2 + place * LOCAL_BINS
        for bit in range(5):
            angle = 2.0 * math.pi * ((first << bit) % PERIOD) / PERIOD
            table[place, 2 * bit] = math.cos(angle)
            table[place, 2 * bit + 1] = math.sin(angle)
    return table.reshape(-1).astype(np.float32)


def inverse_factors():
    n = np.arange(BINS)
    fine = np.exp(2j * np.pi * ((np.arange(32)[:, None] * n) % BINS) / BINS) / math.sqrt(BINS)
    source = np.arange(32)
    first = (source % 4) * 256 + (source // 4) * 32
    coarse = np.exp(2j * np.pi * ((first[:, None] * n) % BINS) / BINS)
    return tuple(part.astype(np.float32) for part in (fine.real, fine.imag, coarse.real, coarse.imag))


def steer(lags, powers, factor):
    re, im = None, None
    for bit in range(5):
        pr, pi = powers[bit]
        chosen = (lags & (1 << bit)) != 0
        if re is None:
            re = jnp.where(chosen, pr * factor, jnp.full(lags.shape, factor, jnp.float32))
            im = jnp.where(chosen, pi * factor, jnp.zeros(lags.shape, jnp.float32))
        else:
            moved_re = re * pr - im * pi
            moved_im = re * pi + im * pr
            re = jnp.where(chosen, moved_re, re)
            im = jnp.where(chosen, moved_im, im)
    return re, im


def begin_steering(place, powers_ref, col_lags_ref, row_lags_ref, col, col_step, row, row_step):
    first = [
        (powers_ref[place * 16 + 2 * bit], powers_ref[place * 16 + 2 * bit + 1]) for bit in range(5)
    ]
    step = [
        (
            np.float32(math.cos(2.0 * math.pi * (1 << bit) / PERIOD)),
            np.float32(math.sin(2.0 * math.pi * (1 << bit) / PERIOD)),
        )
        for bit in range(5)
    ]
    for lags_ref, state, change, count, factor in (
        (col_lags_ref, col, col_step, COLS, COLS**-0.5),
        (row_lags_ref, row, row_step, ROWS, ROWS**-0.5),
    ):

        @pl.loop(0, count // 8)
        def _(group):
            rows = pl.ds(pl.multiple_of(group * 8, 8), 8)
            lags = lags_ref[rows, :]
            re, im = steer(lags, first, np.float32(factor))
            state[rows, 0:BEAMS] = re
            state[rows, BEAMS : 2 * BEAMS] = im
            re, im = steer(lags, step, np.float32(1.0))
            change[rows, 0:BEAMS] = re
            change[rows, BEAMS : 2 * BEAMS] = im


def advance(state, change, rows):
    re = state[rows, 0:BEAMS]
    im = state[rows, BEAMS : 2 * BEAMS]
    cr = change[rows, 0:BEAMS]
    ci = change[rows, BEAMS : 2 * BEAMS]
    state[rows, 0:BEAMS] = re * cr - im * ci
    state[rows, BEAMS : 2 * BEAMS] = re * ci + im * cr
    return re, im


def arrange_sensors(get, sensors):
    low = lax.broadcasted_iota(jnp.int32, (LOCAL_BINS, 128), 1) < 64
    for source in range(8):
        for pair in range(2):
            re = get(0, source, pair).astype(jnp.float32)
            im = get(1, source, pair).astype(jnp.float32)
            row = source * 4 + pair * 2
            sensors[row * 32 : row * 32 + 32, :] = jnp.where(low, re, pltpu.roll(im, 64, 1))
            row = row + 1
            sensors[row * 32 : row * 32 + 32, :] = jnp.where(low, pltpu.roll(re, 64, 1), im)


def beamform_kernel(
    powers_ref, spectra_ref, col_lags_ref, row_lags_ref, out_ref, col, col_step, row, row_step, weights, sensors
):
    place = lax.axis_index("freq") * 8 + lax.axis_index("hyd")
    begin_steering(place, powers_ref, col_lags_ref, row_lags_ref, col, col_step, row, row_step)
    arrange_sensors(
        lambda part, source, pair: spectra_ref[part, source, :, 128 * pair : 128 * pair + 128], sensors
    )

    @pl.loop(0, LOCAL_BINS)
    def _(bin_at):
        for group in range(COLS // 16):
            rows = slice(16 * group, 16 * group + 16)
            re, im = advance(col, col_step, rows)
            weights[rows, 0:BEAMS] = re.astype(jnp.bfloat16)
            weights[rows, BEAMS : 2 * BEAMS] = im.astype(jnp.bfloat16)
            rows = slice(64 + 16 * group, 64 + 16 * group + 16)
            weights[rows, 0:BEAMS] = (-im).astype(jnp.bfloat16)
            weights[rows, BEAMS : 2 * BEAMS] = re.astype(jnp.bfloat16)
        data = sensors[pl.ds(bin_at, 32, stride=32), :].astype(jnp.bfloat16)
        along = jnp.dot(data, weights[...], preferred_element_type=jnp.float32)
        row_re, row_im = advance(row, row_step, slice(0, 32))
        along_re = along[:, 0:BEAMS]
        along_im = along[:, BEAMS:]
        out_ref[pl.ds(bin_at, 1), :] = jnp.sum(along_re * row_re - along_im * row_im, axis=0, keepdims=True)
        out_ref[pl.ds(32 + bin_at, 1), :] = jnp.sum(along_re * row_im + along_im * row_re, axis=0, keepdims=True)


def build_toeplitz(reversed_ref, toeplitz):
    down = lax.broadcasted_iota(jnp.int32, (128, 128), 0)
    across = lax.broadcasted_iota(jnp.int32, (128, 128), 1)
    upper = across >= down

    def circulant(part, tap):
        line = jnp.broadcast_to(reversed_ref[part, pl.ds(tap, 1), :], (128, 128))
        return pltpu.roll(line, 0, 1, stride=1, stride_axis=0)

    @pl.loop(0, TAPS)
    def _(tap):
        rows = pl.ds(pl.multiple_of(tap * 128, 128), 128)
        for part in range(2):
            here = circulant(part, tap)
            after = circulant(part, tap + 1)
            toeplitz[rows, 128 * part : 128 * part + 128] = jnp.where(upper, here, after).astype(jnp.bfloat16)


def build_inverse(fine_re_ref, fine_im_ref, coarse_re_ref, coarse_im_ref, table):
    @pl.loop(0, 32)
    def _(source):
        start = pl.multiple_of(source * 64, 64)
        for half in range(2):
            for block in range(4):
                cols = slice(256 * block, 256 * block + 256)
                fr = fine_re_ref[16 * half : 16 * half + 16, cols]
                fi = fine_im_ref[16 * half : 16 * half + 16, cols]
                cr = coarse_re_ref[pl.ds(source, 1), cols]
                ci = coarse_im_ref[pl.ds(source, 1), cols]
                re = fr * cr - fi * ci
                im = fr * ci + fi * cr
                rows = pl.ds(start + 16 * half, 16)
                table[rows, cols] = re.astype(jnp.bfloat16)
                table[rows, slice(1024 + 256 * block, 1280 + 256 * block)] = im.astype(jnp.bfloat16)
                rows = pl.ds(start + 32 + 16 * half, 16)
                table[rows, cols] = (-im).astype(jnp.bfloat16)
                table[rows, slice(1024 + 256 * block, 1280 + 256 * block)] = re.astype(jnp.bfloat16)


def invert(gathered, table, series):
    series[...] = jnp.zeros_like(series)
    for block in range(8):
        cols = slice(256 * block, 256 * block + 256)
        part, first = block // 4, 2 * (block % 4)
        total = jnp.dot(gathered, table[:, cols], preferred_element_type=jnp.float32)
        for side in range(2):
            series[part, first + side, 0:16, :] = total[:, 128 * side : 128 * side + 128]


def spread(series, blocks):
    for part in range(2):
        for index in range(72):
            ahead, block = index // 8, index % 8
            blocks[part, 16 * index : 16 * index + 16, :] = series[part, block, ahead : ahead + 16, :].astype(
                jnp.bfloat16
            )


def correlate(blocks, toeplitz, total):
    def lines(tap):
        return jnp.concatenate(
            [blocks[part, pl.ds(pl.multiple_of(tap * 16, 16), 128), :] for part in range(2)], axis=0
        )

    last = TAPS - 1
    total[...] = jnp.dot(lines(last), toeplitz[128 * last : 128 * TAPS, :], preferred_element_type=jnp.float32)

    @pl.loop(0, last // 8)
    def _(group):
        tap = group * 8
        data = jnp.concatenate([lines(tap + member) for member in range(8)], axis=1)
        weights = toeplitz[pl.ds(pl.multiple_of(tap * 128, 1024), 1024), :]
        total[...] += jnp.dot(data, weights, preferred_element_type=jnp.float32)


def filter_kernel(
    gathered_ref,
    reversed_ref,
    fine_re_ref,
    fine_im_ref,
    coarse_re_ref,
    coarse_im_ref,
    out_ref,
    toeplitz,
    table,
    series,
    blocks,
    total,
):
    build_toeplitz(reversed_ref, toeplitz)
    build_inverse(fine_re_ref, fine_im_ref, coarse_re_ref, coarse_im_ref, table)
    invert(gathered_ref[...], table, series)
    spread(series, blocks)
    correlate(blocks, toeplitz, total)
    out_ref[0] = total[0:128, 0:128] + total[128:256, 128:256]
    out_ref[1] = total[128:256, 0:128] - total[0:128, 128:256]


def in_vmem(count):
    return [pl.BlockSpec(memory_space=pltpu.VMEM)] * count


def beamform(spectra, col_lags, row_lags):
    return pl.pallas_call(
        beamform_kernel,
        out_shape=jax.ShapeDtypeStruct((64, BEAMS), jnp.float32),
        in_specs=[pl.BlockSpec(memory_space=pltpu.SMEM)] + in_vmem(3),
        out_specs=in_vmem(1)[0],
        scratch_shapes=[
            pltpu.VMEM((COLS, 2 * BEAMS), jnp.float32),
            pltpu.VMEM((COLS, 2 * BEAMS), jnp.float32),
            pltpu.VMEM((ROWS, 2 * BEAMS), jnp.float32),
            pltpu.VMEM((ROWS, 2 * BEAMS), jnp.float32),
            pltpu.VMEM((128, 2 * BEAMS), jnp.bfloat16),
            pltpu.VMEM((1024, 128), jnp.float32),
        ],
    )(jnp.asarray(start_powers()), spectra, col_lags, row_lags)


def matched(gathered, reversed_pulse):
    factors = [jnp.asarray(part) for part in inverse_factors()]
    return pl.pallas_call(
        filter_kernel,
        out_shape=jax.ShapeDtypeStruct((2, 128, 128), jnp.float32),
        in_specs=in_vmem(6),
        out_specs=in_vmem(1)[0],
        scratch_shapes=[
            pltpu.VMEM((TAPS * 128, 256), jnp.bfloat16),
            pltpu.VMEM((2048, 2048), jnp.bfloat16),
            pltpu.VMEM((2, 8, 24, 128), jnp.float32),
            pltpu.VMEM((2, 72 * 16, 128), jnp.bfloat16),
            pltpu.VMEM((256, 256), jnp.float32),
        ],
    )(gathered, reversed_pulse, *factors)


def reverse_pulse(replica, rep_len):
    kept = jnp.arange(REPLICA, dtype=jnp.int32) < rep_len[0]
    masked = jnp.where(kept[None], replica, jnp.zeros_like(replica)).astype(jnp.float32)
    padded = jnp.pad(masked, ((0, 0), (127, (TAPS + 1) * 128 - 127 - REPLICA)))
    return jnp.flip(padded.reshape(2, TAPS + 1, 128), axis=2)


def on_device(spectra, row_lags, col_lags, replica, rep_len):
    moved = lax.all_to_all(
        spectra.reshape(2, 8, LOCAL_BINS, 256), "hyd", split_axis=1, concat_axis=1, tiled=True
    )
    reversed_pulse = reverse_pulse(replica, rep_len)
    formed = beamform(moved, col_lags, row_lags)
    formed = formed.astype(jnp.bfloat16).T
    arrived = lax.all_to_all(formed, ("hyd", "freq"), split_axis=0, concat_axis=0, tiled=True)
    arranged = jnp.transpose(arrived.reshape(32, 16, 64), (1, 0, 2)).reshape(16, 2048)
    gathered = lax.all_to_all(arranged, "tm", split_axis=0, concat_axis=0, tiled=True)
    echoes = matched(gathered, reversed_pulse)
    echoes = jnp.transpose(echoes.reshape(2, 8, 16, 128), (2, 0, 1, 3)).reshape(16, 2 * BINS)
    returned = lax.all_to_all(echoes, "tm", split_axis=0, concat_axis=0, tiled=True)
    return returned.reshape(16, 2, BINS)


def solution(mesh):
    placed = (P(None, "tm", "freq", "hyd"), P(), P(), P(), P())
    return jax.shard_map(
        on_device,
        mesh=mesh,
        in_specs=placed,
        out_specs=P(("hyd", "freq"), None, "tm"),
        check_vma=False,
    )
```

time: 276 us -> 101 us (0.37)
  the two profiles are of different devices: /device:TPU:198 before, /device:TPU:1 now
where the time goes in v1:
time: 101 us; the launch traced here: 99 us
  starting transfers between devices  27.4 us (27%)
  waiting for transfers between devices  25 us (25%)
  Pallas kernels  23.5 us (23%)
  blocking collectives  12.1 us (12%)
  local copies, waits for them, and re-layouts  8 us (8%)
  other arithmetic  2.39 us (2%)
    pallas_call x1, Pallas kernels, matched(): pl.pallas_call(filter_kernel, out_shape=jax.ShapeDtypeStruct((2, 128, 128...  14.1 us
    all_to_all x1, starting transfers between devices, on_device(): lax.all_to_all(arranged, 'tm', split_axis=0, concat_axis=0, tiled=True)  12.4 us
    all_to_all x1, blocking collectives, on_device(): lax.all_to_all(echoes, 'tm', split_axis=0, concat_axis=0, tiled=True)  12.1 us
    pallas_call x1, Pallas kernels, beamform(): pl.pallas_call(beamform_kernel, out_shape=jax.ShapeDtypeStruct((64, BEAMS...  9.38 us
    all_to_all x1, waiting for transfers between devices, on_device(): lax.all_to_all(spectra.reshape(2, 8, LOCAL_BINS, 256), 'hyd', split_axis=...  8.77 us
    all_to_all x1, waiting for transfers between devices, on_device(): lax.all_to_all(formed, ('hyd', 'freq'), split_axis=0, concat_axis=0, tile...  8.24 us
    all_to_all x1, waiting for transfers between devices, on_device(): lax.all_to_all(arranged, 'tm', split_axis=0, concat_axis=0, tiled=True)  7.96 us
    all_to_all x1, starting transfers between devices, on_device(): lax.all_to_all(spectra.reshape(2, 8, LOCAL_BINS, 256), 'hyd', split_axis=...  7.64 us
  transfers between devices with their start and end apart: 3, of which 3 were waited for; matrix products, arithmetic and copies ran while one was open for 1% of the time, Pallas kernels for 0%

profile of v1, /device:TPU:1, one launch (start us, length us, event | category | flops | bytes accessed | tf_op | source)
XLA Modules:
  0.0 99.0 jit_solution(12142489690797644008)
XLA Ops:
  0.0 1.7 %copy.19 = bf16[2,8,32,256]{3,2,0,1:T(8,128)(2,1)} copy(bf16[2,8,32,256]{3,2,1,0:T(8,128)(2,1)} %bitcast.19) | data formatting | bytes 524288 | tf_op jit(solution)/shard_map/reshape | solution.py:281
  1.7 7.6 %all-to-all-start = ((bf16[2,8,32,256]{3,2,0,1:T(8,128)(2,1)}), bf16[2,8,32,256]{3,2,0,1:T(8,128)(2,1)S(1)}, u32[]{:S(2)}, u32[]{:S(2)}) async-start(bf16[2,8,32,256]{3,2,0,1:T(8,128)(2,1)} %copy.19), calls=%async_computation | async-start | bytes 524288 | tf_op jit(solution)/shard_map/all_to_all | solution.py:280
  10.0 8.8 %all-to-all-done = bf16[2,8,32,256]{3,2,0,1:T(8,128)(2,1)S(1)} async-done(((bf16[2,8,32,256]{3,2,0,1:T(8,128)(2,1)}), bf16[2,8,32,256]{3,2,0,1:T(8,128)(2,1)S(1)}, u32[]{:S(2)}, u32[]{:S(2)}) %all-to-all-start) | async-done | bytes 262176 | tf_op jit(solution)/shard_map/all_to_all | solution.py:280
  18.7 0.7 copy.20.spectra_ref
  19.4 9.4 %shard_map.100 = f32[64,512]{1,0:T(8,128)} custom-call(f32[512]{0:T(512)} %constant.15.clone.powers_ref, bf16[2,8,32,256]{3,2,1,0:T(8,128)(2,1)} %copy.20.spectra_ref, s32[64,512]{1,0:T(8,128)} %col_lags_ref.1, s32[32,512]{1,0:T(8,128)} %row_lags_ref.1), custom_call_target="tpu_custom_call" | custom-call | tf_op jit(solution)/shard_map/pallas_call | solution.py:239
  28.8 0.9 convert_bitcast_fusion
  29.7 0.1 copy.21
  29.9 0.8 reshape.41
  30.6 0.0 copy-start
  30.6 7.3 %all-to-all-start.1 = ((bf16[32,2,512]{2,1,0:T(2,128)(2,1)}), bf16[32,2,512]{2,1,0:T(2,128)(2,1)S(1)}, u32[]{:S(2)}, u32[]{:S(2)}) async-start(bf16[32,2,512]{2,1,0:T(2,128)(2,1)} %reshape.41), calls=%async_computation.1 | async-start | bytes 131072 | tf_op jit(solution)/shard_map/all_to_all | solution.py:286
  38.0 0.0 copy-done
  38.0 0.1 broadcast_select_fusion
  38.0 8.2 %all-to-all-done.1 = bf16[32,2,512]{2,1,0:T(2,128)(2,1)S(1)} async-done(((bf16[32,2,512]{2,1,0:T(2,128)(2,1)}), bf16[32,2,512]{2,1,0:T(2,128)(2,1)S(1)}, u32[]{:S(2)}, u32[]{:S(2)}) %all-to-all-start.1) | async-done | bytes 65568 | tf_op jit(solution)/shard_map/all_to_all | solution.py:286
  46.3 0.1 reshape.42
  46.5 0.1 all_to_all.30
  46.6 0.5 broadcast.7
  47.1 1.0 %reduce.1 = bf16[16,2048]{1,0:T(8,128)(2,1)S(1)} reduce(bf16[16,1,2048]{2,1,0:T(2,128)(2,1)S(1)} %all_to_all.30, bf16[]{:T(256)} %broadcast.7), dimensions={1}, to_apply=%all_to_all.30.reduce_sub_computation | reduce | bytes 131074 | tf_op jit(solution)/shard_map/all_to_all | solution.py:288
  48.1 0.7 reshape.43
  48.8 12.4 %all-to-all-start.2 = ((bf16[16,2,1024]{2,1,0:T(2,128)(2,1)}), bf16[16,2,1024]{2,1,0:T(2,128)(2,1)S(1)}, u32[]{:S(2)}, u32[]{:S(2)}) async-start(bf16[16,2,1024]{2,1,0:T(2,128)(2,1)} %reshape.43), calls=%async_computation.2 | async-start | bytes 131072 | tf_op jit(solution)/shard_map/all_to_all | solution.py:288
  61.2 0.1 pad_convert_fusion
  61.3 0.1 reshape.38
  61.3 0.8 rev.4.reversed_ref
  62.1 8.0 %all-to-all-done.2 = bf16[16,2,1024]{2,1,0:T(2,128)(2,1)S(1)} async-done(((bf16[16,2,1024]{2,1,0:T(2,128)(2,1)}), bf16[16,2,1024]{2,1,0:T(2,128)(2,1)S(1)}, u32[]{:S(2)}, u32[]{:S(2)}) %all-to-all-start.2) | async-done | bytes 65568 | tf_op jit(solution)/shard_map/all_to_all | solution.py:288
  70.1 0.1 reshape.44
  70.1 0.7 copy.28
  70.8 14.1 %shard_map.101 = f32[2,128,128]{2,1,0:T(8,128)} custom-call(bf16[16,2048]{1,0:T(8,128)(2,1)} %bitcast.18, f32[2,66,128]{2,1,0:T(8,128)} %rev.4.reversed_ref, f32[32,1024]{1,0:T(8,128)} %constant.16.clone.fine_re_ref, f32[32,1024]{1,0:T(8,128)} %constant.17.clone.fine_im_ref, f32[32,1024]{1,0:T(8,128)} %constant.18.clone.coarse_re_ref, ...), custom_call_target="tpu_custom_call" | custom-call | tf_op jit(solution)/shard_map/pallas_call | solution.py:257
  84.9 0.9 copy.24
  85.9 12.1 %all_to_all.35 = f32[16,1,2048]{2,1,0:T(1,128)S(1)} all-to-all(f32[16,1,2048]{2,1,0:T(1,128)S(1)} %bitcast.17), channel_id=1, replica_groups=mesh['hyd'=8,'tm'=16,'freq'=4] {'tm'}, dimensions={0} | all-to-all | bytes 262144 | tf_op jit(solution)/shard_map/all_to_all | solution.py:291
  98.0 0.3 reduce
  98.3 0.8 reshape.36
  (2 shorter events, 0.0 us)
Async XLA Ops:
  1.7 17.1 %all-to-all-start = ((bf16[2,8,32,256]{3,2,0,1:T(8,128)(2,1)}), bf16[2,8,32,256]{3,2,0,1:T(8,128)(2,1)S(1)}, u32[]{:S(2)}, u32[]{:S(2)}) async-start(bf16[2,8,32,256]{3,2,0,1:T(8,128)(2,1)} %copy.19), calls=%async_computation | async-start | bytes 524288 | tf_op jit(solution)/shard_map/all_to_all | solution.py:280
  30.6 7.3 %copy-start = (bf16[2,8192]{1,0:T(2,128)(2,1)S(1)}, bf16[2,8192]{1,0:T(2,128)(2,1)}, u32[]{:S(2)}) copy-start(bf16[2,8192]{1,0:T(2,128)(2,1)} %param.13) | copy-start | bytes 98308
  30.6 15.7 %all-to-all-start.1 = ((bf16[32,2,512]{2,1,0:T(2,128)(2,1)}), bf16[32,2,512]{2,1,0:T(2,128)(2,1)S(1)}, u32[]{:S(2)}, u32[]{:S(2)}) async-start(bf16[32,2,512]{2,1,0:T(2,128)(2,1)} %reshape.41), calls=%async_computation.1 | async-start | bytes 131072 | tf_op jit(solution)/shard_map/all_to_all | solution.py:286
  48.8 21.3 %all-to-all-start.2 = ((bf16[16,2,1024]{2,1,0:T(2,128)(2,1)}), bf16[16,2,1024]{2,1,0:T(2,128)(2,1)S(1)}, u32[]{:S(2)}, u32[]{:S(2)}) async-start(bf16[16,2,1024]{2,1,0:T(2,128)(2,1)} %reshape.43), calls=%async_computation.2 | async-start | bytes 131072 | tf_op jit(solution)/shard_map/all_to_all | solution.py:288

commit v2 on v1

--- a/solution.py
+++ b/solution.py
@@ -93,63 +93,108 @@
     return re, im
 
 
-def arrange_sensors(get, sensors):
+def arrange_sensors(arrived, sensors):
     low = lax.broadcasted_iota(jnp.int32, (LOCAL_BINS, 128), 1) < 64
     for source in range(8):
         for pair in range(2):
-            re = get(0, source, pair).astype(jnp.float32)
-            im = get(1, source, pair).astype(jnp.float32)
+            cols = slice(128 * pair, 128 * pair + 128)
+            re = arrived[source, 0, :, cols].astype(jnp.float32)
+            im = arrived[source, 1, :, cols].astype(jnp.float32)
             row = source * 4 + pair * 2
             sensors[row * 32 : row * 32 + 32, :] = jnp.where(low, re, pltpu.roll(im, 64, 1))
             row = row + 1
             sensors[row * 32 : row * 32 + 32, :] = jnp.where(low, pltpu.roll(re, 64, 1), im)
 
 
-def beamform_kernel(
-    powers_ref, spectra_ref, col_lags_ref, row_lags_ref, out_ref, col, col_step, row, row_step, weights, sensors
-):
-    place = lax.axis_index("freq") * 8 + lax.axis_index("hyd")
-    begin_steering(place, powers_ref, col_lags_ref, row_lags_ref, col, col_step, row, row_step)
-    arrange_sensors(
-        lambda part, source, pair: spectra_ref[part, source, :, 128 * pair : 128 * pair + 128], sensors
-    )
-
+def build_steering(col, col_step, row, row_step, weights, row_table):
     @pl.loop(0, LOCAL_BINS)
     def _(bin_at):
         for group in range(COLS // 16):
             rows = slice(16 * group, 16 * group + 16)
             re, im = advance(col, col_step, rows)
-            weights[rows, 0:BEAMS] = re.astype(jnp.bfloat16)
-            weights[rows, BEAMS : 2 * BEAMS] = im.astype(jnp.bfloat16)
+            weights[bin_at, rows, 0:BEAMS] = re.astype(jnp.bfloat16)
+            weights[bin_at, rows, BEAMS : 2 * BEAMS] = im.astype(jnp.bfloat16)
             rows = slice(64 + 16 * group, 64 + 16 * group + 16)
-            weights[rows, 0:BEAMS] = (-im).astype(jnp.bfloat16)
-            weights[rows, BEAMS : 2 * BEAMS] = re.astype(jnp.bfloat16)
+            weights[bin_at, rows, 0:BEAMS] = (-im).astype(jnp.bfloat16)
+            weights[bin_at, rows, BEAMS : 2 * BEAMS] = re.astype(jnp.bfloat16)
+        for group in range(ROWS // 8):
+            rows = slice(8 * group, 8 * group + 8)
+            re, im = advance(row, row_step, rows)
+            row_table[bin_at, rows, 0:BEAMS] = re
+            row_table[bin_at, rows, BEAMS : 2 * BEAMS] = im
+
+
+def form_beams(sensors, weights, row_table, formed):
+    formed[64:128, :] = jnp.zeros((64, BEAMS), jnp.float32)
+
+    @pl.loop(0, LOCAL_BINS)
+    def _(bin_at):
         data = sensors[pl.ds(bin_at, 32, stride=32), :].astype(jnp.bfloat16)
-        along = jnp.dot(data, weights[...], preferred_element_type=jnp.float32)
-        row_re, row_im = advance(row, row_step, slice(0, 32))
+        along = jnp.dot(data, weights[bin_at], preferred_element_type=jnp.float32)
+        row_re = row_table[bin_at, :, 0:BEAMS]
+        row_im = row_table[bin_at, :, BEAMS : 2 * BEAMS]
         along_re = along[:, 0:BEAMS]
         along_im = along[:, BEAMS:]
-        out_ref[pl.ds(bin_at, 1), :] = jnp.sum(along_re * row_re - along_im * row_im, axis=0, keepdims=True)
-        out_ref[pl.ds(32 + bin_at, 1), :] = jnp.sum(along_re * row_im + along_im * row_re, axis=0, keepdims=True)
-
-
-def build_toeplitz(reversed_ref, toeplitz):
+        formed[pl.ds(bin_at, 1), :] = jnp.sum(along_re * row_re - along_im * row_im, axis=0, keepdims=True)
+        formed[pl.ds(32 + bin_at, 1), :] = jnp.sum(along_re * row_im + along_im * row_re, axis=0, keepdims=True)
+
+
+def pack_groups(formed, groups):
+    low = lax.broadcasted_iota(jnp.int32, (8, 128), 1) < 64
+    for quarter in range(4):
+        turned = formed[:, 128 * quarter : 128 * quarter + 128].T
+        for member in range(8):
+            first = turned[16 * member : 16 * member + 8]
+            second = turned[16 * member + 8 : 16 * member + 16]
+            packed = jnp.where(low, first, pltpu.roll(second, 64, 1))
+            groups[8 * quarter + member] = packed.astype(jnp.bfloat16)
+
+
+def pack_beams(arrived, work, beams):
+    low = lax.broadcasted_iota(jnp.int32, (8, 128), 1) < 64
+    for pair in range(16):
+        first = arrived[2 * pair].astype(jnp.float32)
+        second = arrived[2 * pair + 1].astype(jnp.float32)
+        work[8 * pair : 8 * pair + 8, :] = jnp.where(low, first, pltpu.roll(second, 64, 1))
+        work[128 + 8 * pair : 136 + 8 * pair, :] = jnp.where(low, pltpu.roll(first, 64, 1), second)
+    for beam in range(16):
+        start = 128 * (beam // 8) + beam % 8
+        beams[beam] = work[pl.ds(start, 16, stride=8), :].astype(jnp.bfloat16)
+
+
+def gather_frames(arrived, work, gathered):
+    for frame in range(FRAMES):
+        work[16 * frame : 16 * frame + 16, :] = arrived[frame].astype(jnp.float32)
+    for pair in range(16):
+        gathered[:, 128 * pair : 128 * pair + 128] = work[pl.ds(pair, 16, stride=16), :].astype(jnp.bfloat16)
+
+
+def lay_pulse(replica, length, lines, mirrored):
+    lines[...] = jnp.zeros_like(lines)
+    lane = lax.broadcasted_iota(jnp.int32, (2, 128), 1)
+    for tap in range(TAPS - 1):
+        line = replica[:, 128 * tap : 128 * tap + 128].astype(jnp.float32)
+        lines[2 + 2 * tap : 4 + 2 * tap, :] = jnp.where(lane + 128 * tap < length, line, 0.0)
     down = lax.broadcasted_iota(jnp.int32, (128, 128), 0)
     across = lax.broadcasted_iota(jnp.int32, (128, 128), 1)
-    upper = across >= down
-
-    def circulant(part, tap):
-        line = jnp.broadcast_to(reversed_ref[part, pl.ds(tap, 1), :], (128, 128))
-        return pltpu.roll(line, 0, 1, stride=1, stride_axis=0)
+    turn = jnp.where((down + across) % 128 == 0, 1.0, 0.0).astype(jnp.bfloat16)
+    mirrored[...] = jnp.dot(lines[...].astype(jnp.bfloat16), turn, preferred_element_type=jnp.float32)
+
+
+def build_toeplitz(mirrored, toeplitz):
+    down = lax.broadcasted_iota(jnp.int32, (128, 128), 0)
+    across = lax.broadcasted_iota(jnp.int32, (128, 128), 1)
+    lower = down >= across
 
     @pl.loop(0, TAPS)
     def _(tap):
         rows = pl.ds(pl.multiple_of(tap * 128, 128), 128)
         for part in range(2):
-            here = circulant(part, tap)
-            after = circulant(part, tap + 1)
-            toeplitz[rows, 128 * part : 128 * part + 128] = jnp.where(upper, here, after).astype(jnp.bfloat16)
-
+            both = []
+            for later in range(2):
+                line = mirrored[pl.ds(2 * tap + 2 * later + part, 1), :]
+                both.append(pltpu.roll(jnp.broadcast_to(line, (128, 128)), 0, 1, stride=1, stride_axis=0))
+            toeplitz[rows, 128 * part : 128 * part + 128] = jnp.where(lower, both[1], both[0]).astype(jnp.bfloat16)
 
 def build_inverse(fine_re_ref, fine_im_ref, coarse_re_ref, coarse_im_ref, table):
     @pl.loop(0, 32)
@@ -208,88 +253,273 @@
         total[...] += jnp.dot(data, weights, preferred_element_type=jnp.float32)
 
 
-def filter_kernel(
-    gathered_ref,
-    reversed_ref,
-    fine_re_ref,
-    fine_im_ref,
-    coarse_re_ref,
-    coarse_im_ref,
-    out_ref,
+def send(source, target, sends, receives, slot, mine, device):
+    return pltpu.make_async_remote_copy(
+        src_ref=source,
+        dst_ref=target,
+        send_sem=sends.at[slot],
+        recv_sem=receives.at[mine],
+        device_id=device,
+        device_id_type=pl.DeviceIdType.MESH,
+    )
+
+
+def ping_kernel(
+    powers_ref,
+    length_ref,
+    spectra_hbm,
+    col_lags_hbm,
+    row_lags_hbm,
+    replica_hbm,
+    factors_hbm,
+    out_hbm,
+    spectra,
+    col_lags,
+    row_lags,
+    replica,
+    factors,
+    arrived_bins,
+    col,
+    col_step,
+    row,
+    row_step,
+    weights,
+    row_table,
+    sensors,
+    formed,
+    groups,
+    arrived_groups,
+    work,
+    beams,
+    arrived_beams,
+    gathered,
+    lines,
+    mirrored,
     toeplitz,
     table,
     series,
     blocks,
     total,
+    leaving,
+    returned,
+    local_sem,
+    bin_send,
+    bin_recv,
+    group_send,
+    group_recv,
+    beam_send,
+    beam_recv,
+    out_send,
+    out_recv,
 ):
-    build_toeplitz(reversed_ref, toeplitz)
-    build_inverse(fine_re_ref, fine_im_ref, coarse_re_ref, coarse_im_ref, table)
-    invert(gathered_ref[...], table, series)
+    hyd = lax.axis_index("hyd")
+    freq = lax.axis_index("freq")
+    tm = lax.axis_index("tm")
+    owner = hyd * 4 + freq
+
+    def owner_at(index):
+        return {"hyd": index // 4, "freq": index % 4}
+
+    barrier = pltpu.get_barrier_semaphore()
+
+    @pl.loop(1, 32)
+    def _(away):
+        pl.semaphore_signal(
+            barrier, inc=1, device_id=owner_at((owner + away) % 32), device_id_type=pl.DeviceIdType.MESH
+        )
+
+    @pl.loop(1, 16)
+    def _(away):
+        pl.semaphore_signal(
+            barrier, inc=1, device_id={"tm": (tm + away) % 16}, device_id_type=pl.DeviceIdType.MESH
+        )
+
+    inputs = [
+        pltpu.make_async_copy(source, target, local_sem.at[index])
+        for index, (source, target) in enumerate(
+            (
+                (col_lags_hbm, col_lags),
+                (row_lags_hbm, row_lags),
+                (spectra_hbm.at[:, 0], spectra),
+                (replica_hbm, replica),
+                (factors_hbm, factors),
+            )
+        )
+    ]
+    for copy in inputs:
+        copy.start()
+    inputs[0].wait()
+    inputs[1].wait()
+    begin_steering(freq * 8 + hyd, powers_ref, col_lags, row_lags, col, col_step, row, row_step)
+    inputs[2].wait()
+    pl.semaphore_wait(barrier, 46)
+
+    def bins_of(place):
+        return spectra.at[:, pl.ds(pl.multiple_of(place * LOCAL_BINS, LOCAL_BINS), LOCAL_BINS), :]
+
+    sent = []
+    for away in (4, 3, 5, 2, 6, 1, 7):
+        place = (hyd + away) % 8
+        copy = send(bins_of(place), arrived_bins.at[hyd], bin_send, bin_recv, away, hyd, {"hyd": place})
+        copy.start()
+        sent.append(copy)
+    own = pltpu.make_async_copy(bins_of(hyd), arrived_bins.at[hyd], local_sem.at[5])
+    own.start()
+
+    build_steering(col, col_step, row, row_step, weights, row_table)
+    inputs[3].wait()
+    inputs[4].wait()
+    lay_pulse(replica, length_ref[0], lines, mirrored)
+    build_toeplitz(mirrored, toeplitz)
+    build_inverse(factors.at[0], factors.at[1], factors.at[2], factors.at[3], table)
+
+    own.wait()
+    for away in range(1, 8):
+        place = (hyd + away) % 8
+        send(bins_of(place), arrived_bins.at[place], bin_send, bin_recv, away, place, {"hyd": place}).wait_recv()
+    arrange_sensors(arrived_bins, sensors)
+    form_beams(sensors, weights, row_table, formed)
+    pack_groups(formed, groups)
+
+    def group_copy(away, source):
+        place = (owner + away) % 32
+        return send(groups.at[place], arrived_groups.at[source], group_send, group_recv, away, source, owner_at(place))
+
+    @pl.loop(1, 32)
+    def _(away):
+        group_copy(away, owner).start()
+
+    own = pltpu.make_async_copy(groups.at[owner], arrived_groups.at[owner], local_sem.at[5])
+    own.start()
+    own.wait()
+
+    @pl.loop(1, 32)
+    def _(away):
+        group_copy(away, (owner + away) % 32).wait_recv()
+
+    pack_beams(arrived_groups, work, beams)
+
+    def beam_copy(away, source):
+        place = (tm + away) % 16
+        return send(beams.at[place], arrived_beams.at[source], beam_send, beam_recv, away, source, {"tm": place})
+
+    @pl.loop(1, 16)
+    def _(away):
+        beam_copy(away, tm).start()
+
+    own = pltpu.make_async_copy(beams.at[tm], arrived_beams.at[tm], local_sem.at[5])
+    own.start()
+    own.wait()
+
+    @pl.loop(1, 16)
+    def _(away):
+        beam_copy(away, (tm + away) % 16).wait_recv()
+
+    gather_frames(arrived_beams, work, gathered)
+    invert(gathered[...], table, series)
     spread(series, blocks)
     correlate(blocks, toeplitz, total)
-    out_ref[0] = total[0:128, 0:128] + total[128:256, 128:256]
-    out_ref[1] = total[128:256, 0:128] - total[0:128, 128:256]
-
-
-def in_vmem(count):
-    return [pl.BlockSpec(memory_space=pltpu.VMEM)] * count
-
-
-def beamform(spectra, col_lags, row_lags):
+    for block in range(8):
+        rows = slice(16 * block, 16 * block + 16)
+        after = slice(128 + 16 * block, 144 + 16 * block)
+        work[pl.ds(block, 16, stride=16), :] = total[rows, 0:128] + total[after, 128:256]
+        work[pl.ds(8 + block, 16, stride=16), :] = total[after, 0:128] - total[rows, 128:256]
+    for frame in range(FRAMES):
+        leaving[frame] = work[16 * frame : 16 * frame + 16, :].astype(jnp.bfloat16)
+
+    def out_copy(away, source):
+        place = (tm + away) % 16
+        return send(leaving.at[place], returned.at[source], out_send, out_recv, away, source, {"tm": place})
+
+    @pl.loop(1, 16)
+    def _(away):
+        out_copy(away, tm).start()
+
+    own = pltpu.make_async_copy(leaving.at[tm], returned.at[tm], local_sem.at[5])
+    own.start()
+    own.wait()
+
+    @pl.loop(1, 16)
+    def _(away):
+        out_copy(away, (tm + away) % 16).wait_recv()
+
+    done = pltpu.make_async_copy(returned, out_hbm, local_sem.at[5])
+    done.start()
+    for copy in sent:
+        copy.wait_send()
+
+    @pl.loop(1, 32)
+    def _(away):
+        group_copy(away, owner).wait_send()
+
+    @pl.loop(1, 16)
+    def _(away):
+        beam_copy(away, tm).wait_send()
+        out_copy(away, tm).wait_send()
+
+    done.wait()
+
+
+def ping(spectra, row_lags, col_lags, replica, rep_len):
+    factors = jnp.asarray(np.stack(inverse_factors()))
+    smem = pl.BlockSpec(memory_space=pltpu.SMEM)
+    hbm = pl.BlockSpec(memory_space=pl.ANY)
+    bf16, f32, i32 = jnp.bfloat16, jnp.float32, jnp.int32
+    dma = pltpu.SemaphoreType.DMA
     return pl.pallas_call(
-        beamform_kernel,
-        out_shape=jax.ShapeDtypeStruct((64, BEAMS), jnp.float32),
-        in_specs=[pl.BlockSpec(memory_space=pltpu.SMEM)] + in_vmem(3),
-        out_specs=in_vmem(1)[0],
+        ping_kernel,
+        out_shape=jax.ShapeDtypeStruct((16, 16, 128), bf16),
+        in_specs=[smem, smem] + [hbm] * 5,
+        out_specs=hbm,
         scratch_shapes=[
-            pltpu.VMEM((COLS, 2 * BEAMS), jnp.float32),
-            pltpu.VMEM((COLS, 2 * BEAMS), jnp.float32),
-            pltpu.VMEM((ROWS, 2 * BEAMS), jnp.float32),
-            pltpu.VMEM((ROWS, 2 * BEAMS), jnp.float32),
-            pltpu.VMEM((128, 2 * BEAMS), jnp.bfloat16),
-            pltpu.VMEM((1024, 128), jnp.float32),
+            pltpu.VMEM((2, 256, 256), bf16),
+            pltpu.VMEM((COLS, BEAMS), i32),
+            pltpu.VMEM((ROWS, BEAMS), i32),
+            pltpu.VMEM((2, REPLICA), bf16),
+            pltpu.VMEM((4, 32, BINS), f32),
+            pltpu.VMEM((8, 2, LOCAL_BINS, 256), bf16),
+            pltpu.VMEM((COLS, 2 * BEAMS), f32),
+            pltpu.VMEM((COLS, 2 * BEAMS), f32),
+            pltpu.VMEM((ROWS, 2 * BEAMS), f32),
+            pltpu.VMEM((ROWS, 2 * BEAMS), f32),
+            pltpu.VMEM((LOCAL_BINS, 128, 2 * BEAMS), bf16),
+            pltpu.VMEM((LOCAL_BINS, ROWS, 2 * BEAMS), f32),
+            pltpu.VMEM((1024, 128), f32),
+            pltpu.VMEM((128, BEAMS), f32),
+            pltpu.VMEM((32, 8, 128), bf16),
+            pltpu.VMEM((32, 8, 128), bf16),
+            pltpu.VMEM((256, 128), f32),
+            pltpu.VMEM((16, 16, 128), bf16),
+            pltpu.VMEM((16, 16, 128), bf16),
+            pltpu.VMEM((16, 2048), bf16),
+            pltpu.VMEM((144, 128), f32),
+            pltpu.VMEM((144, 128), f32),
+            pltpu.VMEM((TAPS * 128, 256), bf16),
+            pltpu.VMEM((2048, 2048), bf16),
+            pltpu.VMEM((2, 8, 24, 128), f32),
+            pltpu.VMEM((2, 72 * 16, 128), bf16),
+            pltpu.VMEM((256, 256), f32),
+            pltpu.VMEM((16, 16, 128), bf16),
+            pltpu.VMEM((16, 16, 128), bf16),
+            dma((6,)),
+            dma((8,)),
+            dma((8,)),
+            dma((32,)),
+            dma((32,)),
+            dma((16,)),
+            dma((16,)),
+            dma((16,)),
+            dma((16,)),
         ],
-    )(jnp.asarray(start_powers()), spectra, col_lags, row_lags)
-
-
-def matched(gathered, reversed_pulse):
-    factors = [jnp.asarray(part) for part in inverse_factors()]
-    return pl.pallas_call(
-        filter_kernel,
-        out_shape=jax.ShapeDtypeStruct((2, 128, 128), jnp.float32),
-        in_specs=in_vmem(6),
-        out_specs=in_vmem(1)[0],
-        scratch_shapes=[
-            pltpu.VMEM((TAPS * 128, 256), jnp.bfloat16),
-            pltpu.VMEM((2048, 2048), jnp.bfloat16),
-            pltpu.VMEM((2, 8, 24, 128), jnp.float32),
-            pltpu.VMEM((2, 72 * 16, 128), jnp.bfloat16),
-            pltpu.VMEM((256, 256), jnp.float32),
-        ],
-    )(gathered, reversed_pulse, *factors)
-
-
-def reverse_pulse(replica, rep_len):
-    kept = jnp.arange(REPLICA, dtype=jnp.int32) < rep_len[0]
-    masked = jnp.where(kept[None], replica, jnp.zeros_like(replica)).astype(jnp.float32)
-    padded = jnp.pad(masked, ((0, 0), (127, (TAPS + 1) * 128 - 127 - REPLICA)))
-    return jnp.flip(padded.reshape(2, TAPS + 1, 128), axis=2)
+        compiler_params=pltpu.CompilerParams(
+            collective_id=0, has_side_effects=True, vmem_limit_bytes=60 * 1024 * 1024
+        ),
+    )(jnp.asarray(start_powers()), rep_len, spectra, col_lags, row_lags, replica, factors)
 
 
 def on_device(spectra, row_lags, col_lags, replica, rep_len):
-    moved = lax.all_to_all(
-        spectra.reshape(2, 8, LOCAL_BINS, 256), "hyd", split_axis=1, concat_axis=1, tiled=True
-    )
-    reversed_pulse = reverse_pulse(replica, rep_len)
-    formed = beamform(moved, col_lags, row_lags)
-    formed = formed.astype(jnp.bfloat16).T
-    arrived = lax.all_to_all(formed, ("hyd", "freq"), split_axis=0, concat_axis=0, tiled=True)
-    arranged = jnp.transpose(arrived.reshape(32, 16, 64), (1, 0, 2)).reshape(16, 2048)
-    gathered = lax.all_to_all(arranged, "tm", split_axis=0, concat_axis=0, tiled=True)
-    echoes = matched(gathered, reversed_pulse)
-    echoes = jnp.transpose(echoes.reshape(2, 8, 16, 128), (2, 0, 1, 3)).reshape(16, 2 * BINS)
-    returned = lax.all_to_all(echoes, "tm", split_axis=0, concat_axis=0, tiled=True)
-    return returned.reshape(16, 2, BINS)
+    returned = ping(spectra, row_lags, col_lags, replica, rep_len)
+    return returned.astype(jnp.float32).reshape(16, 2, BINS)
 
 
 def solution(mesh):

time: 101 us -> 59.7 us (0.59); the launches traced: 99 us -> 59.5 us
  Pallas kernels: 23.5 us -> 57.3 us
  starting transfers between devices: 27.4 us -> 0 us
  waiting for transfers between devices: 25 us -> 0 us
  blocking collectives: 12.1 us -> 0 us
  local copies, waits for them, and re-layouts: 8 us -> 1.56 us
  other arithmetic: 2.39 us -> 0 us
    pallas_call x2 -> x1, Pallas kernels: 23.5 us -> 57.3 us  [ping(): pl.pallas_call(ping_kernel, out_shape=jax.ShapeDtypeStruct((16, 16, 128),...]
    all_to_all x3 -> x0, starting transfers between devices: 27.4 us -> none  [the longest x1 12.4 us: on_device(): lax.all_to_all(arranged, 'tm', split_axis=0, concat_axis=0, tiled=True)]
    all_to_all x3 -> x0, waiting for transfers between devices: 25 us -> none  [the longest x1 8.77 us: on_device(): lax.all_to_all(spectra.reshape(2, 8, LOCAL_BINS, 256), 'hyd', split_axis=...]
    all_to_all x1 -> x0, blocking collectives: 12.1 us -> none  [on_device(): lax.all_to_all(echoes, 'tm', split_axis=0, concat_axis=0, tiled=True)]
    unnamed x7 -> x0, local copies, waits for them, and re-layouts: 2.3 us -> none
    reshape x4 -> x1, local copies, waits for them, and re-layouts: 3.42 us -> 1.56 us  [on_device(): return returned.astype(jnp.float32).reshape(16, 2, BINS)]
    all_to_all x3 -> x0, local copies, waits for them, and re-layouts: 1.33 us -> none  [the longest x1 0.71 us: on_device(): lax.all_to_all(spectra.reshape(2, 8, LOCAL_BINS, 256), 'hyd', split_axis=...]
    all_to_all x2 -> x0, other arithmetic: 1.3 us -> none  [the longest x1 1 us: on_device(): lax.all_to_all(arranged, 'tm', split_axis=0, concat_axis=0, tiled=True)]
  transfers between devices with their start and end apart: 3 -> 0, of which waited for: 3 -> 0; matrix products, arithmetic and copies ran while one was open for 1% -> 0% of each run, Pallas kernels for 0% -> 0%
where the time goes in v2:
time: 59.7 us; the launch traced here: 59.5 us
  Pallas kernels  57.3 us (96%)
  local copies, waits for them, and re-layouts  1.56 us (3%)
  between operations  0.66 us (1%)
    pallas_call x1, Pallas kernels, ping(): pl.pallas_call(ping_kernel, out_shape=jax.ShapeDtypeStruct((16, 16, 128),...  57.3 us
    reshape x1, local copies, waits for them, and re-layouts, on_device(): return returned.astype(jnp.float32).reshape(16, 2, BINS)  1.56 us

profile of v2, /device:TPU:1, one launch (start us, length us, event | category | flops | bytes accessed | tf_op | source)
XLA Modules:
  0.0 59.5 jit_solution(10507948912000308436)
XLA Ops:
  0.7 57.3 %shard_map.73 = bf16[16,16,128]{2,1,0:T(8,128)(2,1)} custom-call(f32[512]{0:T(512)} %constant.5.clone.powers_ref, s32[1]{0:T(128)S(6)} %copy.8.length_ref, bf16[2,1,256,256]{3,2,1,0:T(8,128)(2,1)} %spectra_hbm.1, s32[64,512]{1,0:T(8,128)} %col_lags_hbm.1, s32[32,512]{1,0:T(8,128)} %row_lags_hbm.1, bf16[2,8192]{1,0:T(2,128)(2,1)} %replica_hbm.1, ...), custom_call_target="tpu_custom_call" | custom-call | tf_op jit(solution)/shard_map/pallas_call | solution.py:469
  57.9 1.6 %reshape.9 = f32[16,2,1024]{2,1,0:T(2,128)} reshape(bf16[16,16,128]{2,1,0:T(8,128)(2,1)} %shard_map.73) | data formatting | bytes 196608 | tf_op jit(solution)/shard_map/reshape | solution.py:522

commit v3 on v2

--- a/solution.py
+++ b/solution.py
@@ -1,3 +1,4 @@
+import functools
 import math
 
 import jax
@@ -127,7 +128,7 @@
 def form_beams(sensors, weights, row_table, formed):
     formed[64:128, :] = jnp.zeros((64, BEAMS), jnp.float32)
 
-    @pl.loop(0, LOCAL_BINS)
+    @pl.loop(0, LOCAL_BINS, unroll=4)
     def _(bin_at):
         data = sensors[pl.ds(bin_at, 32, stride=32), :].astype(jnp.bfloat16)
         along = jnp.dot(data, weights[bin_at], preferred_element_type=jnp.float32)
@@ -141,8 +142,10 @@
 
 def pack_groups(formed, groups):
     low = lax.broadcasted_iota(jnp.int32, (8, 128), 1) < 64
-    for quarter in range(4):
-        turned = formed[:, 128 * quarter : 128 * quarter + 128].T
+
+    @pl.loop(0, 4)
+    def _(quarter):
+        turned = formed[:, pl.ds(pl.multiple_of(128 * quarter, 128), 128)].T
         for member in range(8):
             first = turned[16 * member : 16 * member + 8]
             second = turned[16 * member + 8 : 16 * member + 16]
@@ -186,15 +189,19 @@
     across = lax.broadcasted_iota(jnp.int32, (128, 128), 1)
     lower = down >= across
 
-    @pl.loop(0, TAPS)
-    def _(tap):
-        rows = pl.ds(pl.multiple_of(tap * 128, 128), 128)
-        for part in range(2):
-            both = []
-            for later in range(2):
-                line = mirrored[pl.ds(2 * tap + 2 * later + part, 1), :]
-                both.append(pltpu.roll(jnp.broadcast_to(line, (128, 128)), 0, 1, stride=1, stride_axis=0))
-            toeplitz[rows, 128 * part : 128 * part + 128] = jnp.where(lower, both[1], both[0]).astype(jnp.bfloat16)
+    def circulant(row):
+        line = jnp.broadcast_to(mirrored[pl.ds(row, 1), :], (128, 128))
+        return pltpu.roll(line, 0, 1, stride=1, stride_axis=0)
+
+    for part in range(2):
+
+        @functools.partial(lax.fori_loop, 0, TAPS, init_val=circulant(part))
+        def _(tap, before):
+            rows = pl.ds(pl.multiple_of(tap * 128, 128), 128)
+            here = circulant(2 * tap + 2 + part)
+            toeplitz[rows, 128 * part : 128 * part + 128] = jnp.where(lower, here, before).astype(jnp.bfloat16)
+            return here
+
 
 def build_inverse(fine_re_ref, fine_im_ref, coarse_re_ref, coarse_im_ref, table):
     @pl.loop(0, 32)
@@ -219,12 +226,13 @@
 
 def invert(gathered, table, series):
     series[...] = jnp.zeros_like(series)
-    for block in range(8):
-        cols = slice(256 * block, 256 * block + 256)
-        part, first = block // 4, 2 * (block % 4)
-        total = jnp.dot(gathered, table[:, cols], preferred_element_type=jnp.float32)
+
+    @pl.loop(0, 8)
+    def _(block):
+        cols = pl.ds(pl.multiple_of(256 * block, 256), 256)
+        total = jnp.dot(gathered[...], table[:, cols], preferred_element_type=jnp.float32)
         for side in range(2):
-            series[part, first + side, 0:16, :] = total[:, 128 * side : 128 * side + 128]
+            series[block // 4, 2 * (block % 4) + side, 0:16, :] = total[:, 128 * side : 128 * side + 128]
 
 
 def spread(series, blocks):
@@ -253,12 +261,31 @@
         total[...] += jnp.dot(data, weights, preferred_element_type=jnp.float32)
 
 
-def send(source, target, sends, receives, slot, mine, device):
+def pack_echoes(total, work, leaving):
+    for block in range(8):
+        rows = slice(16 * block, 16 * block + 16)
+        after = slice(128 + 16 * block, 144 + 16 * block)
+        work[pl.ds(2 * block, 16, stride=16), :] = total[rows, 0:128] + total[after, 128:256]
+        work[pl.ds(2 * block + 1, 16, stride=16), :] = total[after, 0:128] - total[rows, 128:256]
+    for frame in range(FRAMES):
+        leaving[frame] = work[16 * frame : 16 * frame + 16, :].astype(jnp.bfloat16)
+
+
+def unpack_echoes(returned, work):
+    for beam in range(16):
+        work[16 * beam : 16 * beam + 16, :] = returned[beam].astype(jnp.float32)
+
+
+RING8 = (4, 3, 5, 2, 6, 1, 7, 0)
+RING4 = (2, 1, 3, 0)
+
+
+def send(source, target, sends, receives, slot, device):
     return pltpu.make_async_remote_copy(
         src_ref=source,
         dst_ref=target,
         send_sem=sends.at[slot],
-        recv_sem=receives.at[mine],
+        recv_sem=receives.at[slot],
         device_id=device,
         device_id_type=pl.DeviceIdType.MESH,
     )
@@ -317,55 +344,59 @@
     tm = lax.axis_index("tm")
     owner = hyd * 4 + freq
 
-    def owner_at(index):
-        return {"hyd": index // 4, "freq": index % 4}
-
-    barrier = pltpu.get_barrier_semaphore()
-
-    @pl.loop(1, 32)
-    def _(away):
-        pl.semaphore_signal(
-            barrier, inc=1, device_id=owner_at((owner + away) % 32), device_id_type=pl.DeviceIdType.MESH
-        )
-
-    @pl.loop(1, 16)
-    def _(away):
-        pl.semaphore_signal(
-            barrier, inc=1, device_id={"tm": (tm + away) % 16}, device_id_type=pl.DeviceIdType.MESH
-        )
-
     inputs = [
         pltpu.make_async_copy(source, target, local_sem.at[index])
         for index, (source, target) in enumerate(
             (
+                (spectra_hbm.at[:, 0], spectra),
                 (col_lags_hbm, col_lags),
                 (row_lags_hbm, row_lags),
-                (spectra_hbm.at[:, 0], spectra),
                 (replica_hbm, replica),
                 (factors_hbm, factors),
             )
         )
     ]
-    for copy in inputs:
+    inputs[0].start()
+
+    owners = []
+    for ahead in RING8:
+        for side in range(4):
+            if ahead or side:
+                to = ((hyd + ahead) & 7, (freq + side) & 3)
+                back = ((hyd - ahead) & 7, (freq - side) & 3)
+                owners.append((ahead * 4 + side, to[0] * 4 + to[1], back[0] * 4 + back[1], {"hyd": to[0], "freq": to[1]}))
+    frames = []
+    for far in RING4:
+        for near in RING4:
+            if far or near:
+                to = ((((tm >> 2) + far) & 3) * 4) + ((tm + near) & 3)
+                back = ((((tm >> 2) - far) & 3) * 4) + ((tm - near) & 3)
+                frames.append((far * 4 + near, to, back, {"tm": to}))
+
+    barrier = pltpu.get_barrier_semaphore()
+    for _, _, _, device in owners + frames:
+        pl.semaphore_signal(barrier, inc=1, device_id=device, device_id_type=pl.DeviceIdType.MESH)
+
+    for copy in inputs[1:]:
         copy.start()
     inputs[0].wait()
-    inputs[1].wait()
-    begin_steering(freq * 8 + hyd, powers_ref, col_lags, row_lags, col, col_step, row, row_step)
-    inputs[2].wait()
     pl.semaphore_wait(barrier, 46)
 
     def bins_of(place):
         return spectra.at[:, pl.ds(pl.multiple_of(place * LOCAL_BINS, LOCAL_BINS), LOCAL_BINS), :]
 
-    sent = []
-    for away in (4, 3, 5, 2, 6, 1, 7):
-        place = (hyd + away) % 8
-        copy = send(bins_of(place), arrived_bins.at[hyd], bin_send, bin_recv, away, hyd, {"hyd": place})
-        copy.start()
-        sent.append(copy)
+    def bin_copy(ahead, source):
+        place = (hyd + ahead) & 7
+        return send(bins_of(place), arrived_bins.at[source], bin_send, bin_recv, ahead, {"hyd": place})
+
+    for ahead in RING8[:-1]:
+        bin_copy(ahead, hyd).start()
     own = pltpu.make_async_copy(bins_of(hyd), arrived_bins.at[hyd], local_sem.at[5])
     own.start()
 
+    inputs[1].wait()
+    inputs[2].wait()
+    begin_steering(freq * 8 + hyd, powers_ref, col_lags, row_lags, col, col_step, row, row_step)
     build_steering(col, col_step, row, row_step, weights, row_table)
     inputs[3].wait()
     inputs[4].wait()
@@ -374,89 +405,46 @@
     build_inverse(factors.at[0], factors.at[1], factors.at[2], factors.at[3], table)
 
     own.wait()
-    for away in range(1, 8):
-        place = (hyd + away) % 8
-        send(bins_of(place), arrived_bins.at[place], bin_send, bin_recv, away, place, {"hyd": place}).wait_recv()
+    for ahead in RING8[-2::-1]:
+        bin_copy(ahead, (hyd - ahead) & 7).wait_recv()
     arrange_sensors(arrived_bins, sensors)
     form_beams(sensors, weights, row_table, formed)
     pack_groups(formed, groups)
 
-    def group_copy(away, source):
-        place = (owner + away) % 32
-        return send(groups.at[place], arrived_groups.at[source], group_send, group_recv, away, source, owner_at(place))
-
-    @pl.loop(1, 32)
-    def _(away):
-        group_copy(away, owner).start()
-
-    own = pltpu.make_async_copy(groups.at[owner], arrived_groups.at[owner], local_sem.at[5])
-    own.start()
-    own.wait()
-
-    @pl.loop(1, 32)
-    def _(away):
-        group_copy(away, (owner + away) % 32).wait_recv()
-
+    def exchange(peers, mine, leaves, arrives, sends, receives):
+        def copy(slot, place, source, device):
+            return send(leaves.at[place], arrives.at[source], sends, receives, slot, device)
+
+        for slot, place, _, device in peers:
+            copy(slot, place, mine, device).start()
+        own = pltpu.make_async_copy(leaves.at[mine], arrives.at[mine], local_sem.at[5])
+        own.start()
+        own.wait()
+        for slot, place, source, device in peers[::-1]:
+            copy(slot, place, source, device).wait_recv()
+
+    def drain(peers, mine, leaves, arrives, sends, receives):
+        for slot, place, _, device in peers:
+            send(leaves.at[place], arrives.at[mine], sends, receives, slot, device).wait_send()
+
+    exchange(owners, owner, groups, arrived_groups, group_send, group_recv)
     pack_beams(arrived_groups, work, beams)
-
-    def beam_copy(away, source):
-        place = (tm + away) % 16
-        return send(beams.at[place], arrived_beams.at[source], beam_send, beam_recv, away, source, {"tm": place})
-
-    @pl.loop(1, 16)
-    def _(away):
-        beam_copy(away, tm).start()
-
-    own = pltpu.make_async_copy(beams.at[tm], arrived_beams.at[tm], local_sem.at[5])
-    own.start()
-    own.wait()
-
-    @pl.loop(1, 16)
-    def _(away):
-        beam_copy(away, (tm + away) % 16).wait_recv()
-
+    exchange(frames, tm, beams, arrived_beams, beam_send, beam_recv)
     gather_frames(arrived_beams, work, gathered)
-    invert(gathered[...], table, series)
+    invert(gathered, table, series)
     spread(series, blocks)
     correlate(blocks, toeplitz, total)
-    for block in range(8):
-        rows = slice(16 * block, 16 * block + 16)
-        after = slice(128 + 16 * block, 144 + 16 * block)
-        work[pl.ds(block, 16, stride=16), :] = total[rows, 0:128] + total[after, 128:256]
-        work[pl.ds(8 + block, 16, stride=16), :] = total[after, 0:128] - total[rows, 128:256]
-    for frame in range(FRAMES):
-        leaving[frame] = work[16 * frame : 16 * frame + 16, :].astype(jnp.bfloat16)
-
-    def out_copy(away, source):
-        place = (tm + away) % 16
-        return send(leaving.at[place], returned.at[source], out_send, out_recv, away, source, {"tm": place})
-
-    @pl.loop(1, 16)
-    def _(away):
-        out_copy(away, tm).start()
-
-    own = pltpu.make_async_copy(leaving.at[tm], returned.at[tm], local_sem.at[5])
-    own.start()
-    own.wait()
-
-    @pl.loop(1, 16)
-    def _(away):
-        out_copy(away, (tm + away) % 16).wait_recv()
-
-    done = pltpu.make_async_copy(returned, out_hbm, local_sem.at[5])
+    pack_echoes(total, work, leaving)
+    exchange(frames, tm, leaving, returned, out_send, out_recv)
+    unpack_echoes(returned, work)
+
+    done = pltpu.make_async_copy(work, out_hbm, local_sem.at[5])
     done.start()
-    for copy in sent:
-        copy.wait_send()
-
-    @pl.loop(1, 32)
-    def _(away):
-        group_copy(away, owner).wait_send()
-
-    @pl.loop(1, 16)
-    def _(away):
-        beam_copy(away, tm).wait_send()
-        out_copy(away, tm).wait_send()
-
+    for ahead in RING8[:-1]:
+        bin_copy(ahead, hyd).wait_send()
+    drain(owners, owner, groups, arrived_groups, group_send, group_recv)
+    drain(frames, tm, beams, arrived_beams, beam_send, beam_recv)
+    drain(frames, tm, leaving, returned, out_send, out_recv)
     done.wait()
 
 
@@ -468,7 +456,7 @@
     dma = pltpu.SemaphoreType.DMA
     return pl.pallas_call(
         ping_kernel,
-        out_shape=jax.ShapeDtypeStruct((16, 16, 128), bf16),
+        out_shape=jax.ShapeDtypeStruct((256, 128), f32),
         in_specs=[smem, smem] + [hbm] * 5,
         out_specs=hbm,
         scratch_shapes=[
@@ -519,7 +507,7 @@
 
 def on_device(spectra, row_lags, col_lags, replica, rep_len):
     returned = ping(spectra, row_lags, col_lags, replica, rep_len)
-    return returned.astype(jnp.float32).reshape(16, 2, BINS)
+    return jnp.transpose(returned.reshape(16, 8, 2, 128), (0, 2, 1, 3)).reshape(16, 2, BINS)
 
 
 def solution(mesh):

time: 59.7 us -> 61.1 us (1.023)
  Pallas kernels: 57.3 us -> 58.7 us
    unnamed x0 -> x1, local copies, waits for them, and re-layouts: none -> 1.57 us
    reshape x1 -> x0, local copies, waits for them, and re-layouts: 1.56 us -> none  [on_device(): return returned.astype(jnp.float32).reshape(16, 2, BINS)]
    pallas_call x1, Pallas kernels: 57.3 us -> 58.7 us  [ping(): pl.pallas_call(ping_kernel, out_shape=jax.ShapeDtypeStruct((256, 128), f3...]
where the time goes in v3:
time: 61.1 us; the launch traced here: 60.9 us
  Pallas kernels  58.7 us (96%)
  local copies, waits for them, and re-layouts  1.57 us (3%)
  between operations  0.66 us (1%)
    pallas_call x1, Pallas kernels, ping(): pl.pallas_call(ping_kernel, out_shape=jax.ShapeDtypeStruct((256, 128), f3...  58.7 us
    unnamed x1, local copies, waits for them, and re-layouts  1.57 us

profile of v3, /device:TPU:1, one launch (start us, length us, event | category | flops | bytes accessed | tf_op | source)
XLA Modules:
  0.0 60.9 jit_solution(3723881041682213242)
XLA Ops:
  0.7 58.7 %shard_map.73 = f32[256,128]{1,0:T(8,128)} custom-call(f32[512]{0:T(512)} %constant.5.clone.powers_ref, s32[1]{0:T(128)S(6)} %copy.10.length_ref, bf16[2,1,256,256]{3,2,1,0:T(8,128)(2,1)} %spectra_hbm.1, s32[64,512]{1,0:T(8,128)} %col_lags_hbm.1, s32[32,512]{1,0:T(8,128)} %row_lags_hbm.1, bf16[2,8192]{1,0:T(2,128)(2,1)} %replica_hbm.1, ...), custom_call_target="tpu_custom_call" | custom-call | tf_op jit(solution)/shard_map/pallas_call | solution.py:457
  59.3 1.6 %copy.11 = f32[16,2,1024]{2,1,0:T(2,128)} copy(f32[16,2,1024]{2,1,0:T(2,128)} %bitcast.5) | data formatting | bytes 262144

commit v4 on v3

--- a/solution.py
+++ b/solution.py
@@ -189,18 +189,17 @@
     across = lax.broadcasted_iota(jnp.int32, (128, 128), 1)
     lower = down >= across
 
-    def circulant(row):
-        line = jnp.broadcast_to(mirrored[pl.ds(row, 1), :], (128, 128))
-        return pltpu.roll(line, 0, 1, stride=1, stride_axis=0)
-
-    for part in range(2):
-
-        @functools.partial(lax.fori_loop, 0, TAPS, init_val=circulant(part))
-        def _(tap, before):
-            rows = pl.ds(pl.multiple_of(tap * 128, 128), 128)
-            here = circulant(2 * tap + 2 + part)
-            toeplitz[rows, 128 * part : 128 * part + 128] = jnp.where(lower, here, before).astype(jnp.bfloat16)
-            return here
+    @pl.loop(0, TAPS // 5)
+    def _(group):
+        for part in range(2):
+            turned = []
+            for member in range(6):
+                line = mirrored[pl.ds(2 * (group * 5 + member) + part, 1), :]
+                turned.append(pltpu.roll(jnp.broadcast_to(line, (128, 128)), 0, 1, stride=1, stride_axis=0))
+            for member in range(5):
+                rows = pl.ds(pl.multiple_of((group * 5 + member) * 128, 128), 128)
+                both = jnp.where(lower, turned[member + 1], turned[member])
+                toeplitz[rows, 128 * part : 128 * part + 128] = both.astype(jnp.bfloat16)
 
 
 def build_inverse(fine_re_ref, fine_im_ref, coarse_re_ref, coarse_im_ref, table):
@@ -227,12 +226,12 @@
 def invert(gathered, table, series):
     series[...] = jnp.zeros_like(series)
 
-    @pl.loop(0, 8)
+    @pl.loop(0, 4)
     def _(block):
-        cols = pl.ds(pl.multiple_of(256 * block, 256), 256)
+        cols = pl.ds(pl.multiple_of(512 * block, 512), 512)
         total = jnp.dot(gathered[...], table[:, cols], preferred_element_type=jnp.float32)
-        for side in range(2):
-            series[block // 4, 2 * (block % 4) + side, 0:16, :] = total[:, 128 * side : 128 * side + 128]
+        for side in range(4):
+            series[block // 2, 4 * (block % 2) + side, 0:16, :] = total[:, 128 * side : 128 * side + 128]
 
 
 def spread(series, blocks):
@@ -253,11 +252,11 @@
     last = TAPS - 1
     total[...] = jnp.dot(lines(last), toeplitz[128 * last : 128 * TAPS, :], preferred_element_type=jnp.float32)
 
-    @pl.loop(0, last // 8)
+    @pl.loop(0, last // 16)
     def _(group):
-        tap = group * 8
-        data = jnp.concatenate([lines(tap + member) for member in range(8)], axis=1)
-        weights = toeplitz[pl.ds(pl.multiple_of(tap * 128, 1024), 1024), :]
+        tap = group * 16
+        data = jnp.concatenate([lines(tap + member) for member in range(16)], axis=1)
+        weights = toeplitz[pl.ds(pl.multiple_of(tap * 128, 16 * 128), 16 * 128), :]
         total[...] += jnp.dot(data, weights, preferred_element_type=jnp.float32)
 
 

time: 61.1 us -> 51.3 us (0.84)
  Pallas kernels: 58.7 us -> 48.9 us
    pallas_call x1, Pallas kernels: 58.7 us -> 48.9 us  [ping(): pl.pallas_call(ping_kernel, out_shape=jax.ShapeDtypeStruct((256, 128), f3...]
where the time goes in v4:
time: 51.3 us; the launch traced here: 51.2 us
  Pallas kernels  48.9 us (95%)
  local copies, waits for them, and re-layouts  1.57 us (3%)
  between operations  0.66 us (1%)
    pallas_call x1, Pallas kernels, ping(): pl.pallas_call(ping_kernel, out_shape=jax.ShapeDtypeStruct((256, 128), f3...  48.9 us
    unnamed x1, local copies, waits for them, and re-layouts  1.57 us

profile of v4, /device:TPU:1, one launch (start us, length us, event | category | flops | bytes accessed | tf_op | source)
XLA Modules:
  0.0 51.2 jit_solution(18272549253358518006)
XLA Ops:
  0.7 48.9 %shard_map.73 = f32[256,128]{1,0:T(8,128)} custom-call(f32[512]{0:T(512)} %constant.5.clone.powers_ref, s32[1]{0:T(128)S(6)} %copy.10.length_ref, bf16[2,1,256,256]{3,2,1,0:T(8,128)(2,1)} %spectra_hbm.1, s32[64,512]{1,0:T(8,128)} %col_lags_hbm.1, s32[32,512]{1,0:T(8,128)} %row_lags_hbm.1, bf16[2,8192]{1,0:T(2,128)(2,1)} %replica_hbm.1, ...), custom_call_target="tpu_custom_call" | custom-call | tf_op jit(solution)/shard_map/pallas_call | solution.py:456
  49.6 1.6 %copy.11 = f32[16,2,1024]{2,1,0:T(2,128)} copy(f32[16,2,1024]{2,1,0:T(2,128)} %bitcast.5) | data formatting | bytes 262144

commit v5 on v4

--- a/solution.py
+++ b/solution.py
@@ -17,6 +17,7 @@
 REPLICA = 8192
 PERIOD = 2 * BINS
 LOCAL_BINS = 32
+HALF = LOCAL_BINS // 2
 TAPS = REPLICA // 128 + 1
 
 
@@ -94,17 +95,18 @@
     return re, im
 
 
-def arrange_sensors(arrived, sensors):
-    low = lax.broadcasted_iota(jnp.int32, (LOCAL_BINS, 128), 1) < 64
+def arrange_sensors(arrived, sensors, half):
+    low = lax.broadcasted_iota(jnp.int32, (HALF, 128), 1) < 64
+    bins = pl.ds(pl.multiple_of(half * HALF, HALF), HALF)
     for source in range(8):
         for pair in range(2):
             cols = slice(128 * pair, 128 * pair + 128)
-            re = arrived[source, 0, :, cols].astype(jnp.float32)
-            im = arrived[source, 1, :, cols].astype(jnp.float32)
+            re = arrived[source, 0, bins, cols].astype(jnp.float32)
+            im = arrived[source, 1, bins, cols].astype(jnp.float32)
             row = source * 4 + pair * 2
-            sensors[row * 32 : row * 32 + 32, :] = jnp.where(low, re, pltpu.roll(im, 64, 1))
-            row = row + 1
-            sensors[row * 32 : row * 32 + 32, :] = jnp.where(low, pltpu.roll(re, 64, 1), im)
+            start = pl.multiple_of(half * HALF, HALF)
+            sensors[pl.ds(row * 32 + start, HALF), :] = jnp.where(low, re, pltpu.roll(im, 64, 1))
+            sensors[pl.ds(row * 32 + 32 + start, HALF), :] = jnp.where(low, pltpu.roll(re, 64, 1), im)
 
 
 def build_steering(col, col_step, row, row_step, weights, row_table):
@@ -125,11 +127,10 @@
             row_table[bin_at, rows, BEAMS : 2 * BEAMS] = im
 
 
-def form_beams(sensors, weights, row_table, formed):
-    formed[64:128, :] = jnp.zeros((64, BEAMS), jnp.float32)
-
-    @pl.loop(0, LOCAL_BINS, unroll=4)
-    def _(bin_at):
+def form_beams(sensors, weights, row_table, formed, half):
+    @pl.loop(0, HALF, unroll=4)
+    def _(step):
+        bin_at = half * HALF + step
         data = sensors[pl.ds(bin_at, 32, stride=32), :].astype(jnp.bfloat16)
         along = jnp.dot(data, weights[bin_at], preferred_element_type=jnp.float32)
         row_re = row_table[bin_at, :, 0:BEAMS]
@@ -337,6 +338,7 @@
     beam_recv,
     out_send,
     out_recv,
+    relayed,
 ):
     hyd = lax.axis_index("hyd")
     freq = lax.axis_index("freq")
@@ -373,44 +375,60 @@
                 frames.append((far * 4 + near, to, back, {"tm": to}))
 
     barrier = pltpu.get_barrier_semaphore()
-    for _, _, _, device in owners + frames:
+    beside = [{"freq": (freq + side) & 3} for side in range(1, 4)]
+    near = [{"tm": (tm & 12) + ((tm + step) & 3)} for step in range(1, 4)]
+    along = [{"hyd": (hyd + ahead) & 7} for ahead in RING8[:-1]]
+    across = [{"tm": (tm + 4 * step) & 15} for step in range(1, 4)]
+    for device in along + across + near + beside:
         pl.semaphore_signal(barrier, inc=1, device_id=device, device_id_type=pl.DeviceIdType.MESH)
 
     for copy in inputs[1:]:
         copy.start()
     inputs[0].wait()
-    pl.semaphore_wait(barrier, 46)
-
-    def bins_of(place):
-        return spectra.at[:, pl.ds(pl.multiple_of(place * LOCAL_BINS, LOCAL_BINS), LOCAL_BINS), :]
-
-    def bin_copy(ahead, source):
+    pl.semaphore_wait(barrier, 16)
+
+    def bin_copy(half, ahead, source):
         place = (hyd + ahead) & 7
-        return send(bins_of(place), arrived_bins.at[source], bin_send, bin_recv, ahead, {"hyd": place})
-
-    for ahead in RING8[:-1]:
-        bin_copy(ahead, hyd).start()
-    own = pltpu.make_async_copy(bins_of(hyd), arrived_bins.at[hyd], local_sem.at[5])
+        start = pl.multiple_of(place * LOCAL_BINS + half * HALF, HALF)
+        bins = pl.ds(pl.multiple_of(half * HALF, HALF), HALF)
+        return send(
+            spectra.at[:, pl.ds(start, HALF), :],
+            arrived_bins.at[source, :, bins, :],
+            bin_send,
+            bin_recv,
+            half * 8 + ahead,
+            {"hyd": place},
+        )
+
+    for half in range(2):
+        for ahead in RING8[:-1]:
+            bin_copy(half, ahead, hyd).start()
+    mine = pl.ds(pl.multiple_of(hyd * LOCAL_BINS, LOCAL_BINS), LOCAL_BINS)
+    own = pltpu.make_async_copy(spectra.at[:, mine, :], arrived_bins.at[hyd], local_sem.at[5])
     own.start()
+    for device in near + beside:
+        pl.semaphore_signal(relayed, inc=1, device_id=device, device_id_type=pl.DeviceIdType.MESH)
 
     inputs[1].wait()
     inputs[2].wait()
     begin_steering(freq * 8 + hyd, powers_ref, col_lags, row_lags, col, col_step, row, row_step)
     build_steering(col, col_step, row, row_step, weights, row_table)
     inputs[3].wait()
-    inputs[4].wait()
     lay_pulse(replica, length_ref[0], lines, mirrored)
-    build_toeplitz(mirrored, toeplitz)
-    build_inverse(factors.at[0], factors.at[1], factors.at[2], factors.at[3], table)
-
+    formed[64:128, :] = jnp.zeros((64, BEAMS), jnp.float32)
     own.wait()
-    for ahead in RING8[-2::-1]:
-        bin_copy(ahead, (hyd - ahead) & 7).wait_recv()
-    arrange_sensors(arrived_bins, sensors)
-    form_beams(sensors, weights, row_table, formed)
+
+    @pl.loop(0, 2)
+    def _(half):
+        for ahead in RING8[-2::-1]:
+            bin_copy(half, ahead, (hyd - ahead) & 7).wait_recv()
+        arrange_sensors(arrived_bins, sensors, half)
+        form_beams(sensors, weights, row_table, formed, half)
+
     pack_groups(formed, groups)
-
-    def exchange(peers, mine, leaves, arrives, sends, receives):
+    pl.semaphore_wait(relayed, 6)
+
+    def exchange(peers, mine, leaves, arrives, sends, receives, meanwhile=None):
         def copy(slot, place, source, device):
             return send(leaves.at[place], arrives.at[source], sends, receives, slot, device)
 
@@ -418,6 +436,8 @@
             copy(slot, place, mine, device).start()
         own = pltpu.make_async_copy(leaves.at[mine], arrives.at[mine], local_sem.at[5])
         own.start()
+        if meanwhile is not None:
+            meanwhile()
         own.wait()
         for slot, place, source, device in peers[::-1]:
             copy(slot, place, source, device).wait_recv()
@@ -426,7 +446,12 @@
         for slot, place, _, device in peers:
             send(leaves.at[place], arrives.at[mine], sends, receives, slot, device).wait_send()
 
-    exchange(owners, owner, groups, arrived_groups, group_send, group_recv)
+    def build_tables():
+        inputs[4].wait()
+        build_toeplitz(mirrored, toeplitz)
+        build_inverse(factors.at[0], factors.at[1], factors.at[2], factors.at[3], table)
+
+    exchange(owners, owner, groups, arrived_groups, group_send, group_recv, build_tables)
     pack_beams(arrived_groups, work, beams)
     exchange(frames, tm, beams, arrived_beams, beam_send, beam_recv)
     gather_frames(arrived_beams, work, gathered)
@@ -439,8 +464,9 @@
 
     done = pltpu.make_async_copy(work, out_hbm, local_sem.at[5])
     done.start()
-    for ahead in RING8[:-1]:
-        bin_copy(ahead, hyd).wait_send()
+    for half in range(2):
+        for ahead in RING8[:-1]:
+            bin_copy(half, ahead, hyd).wait_send()
     drain(owners, owner, groups, arrived_groups, group_send, group_recv)
     drain(frames, tm, beams, arrived_beams, beam_send, beam_recv)
     drain(frames, tm, leaving, returned, out_send, out_recv)
@@ -489,14 +515,15 @@
             pltpu.VMEM((16, 16, 128), bf16),
             pltpu.VMEM((16, 16, 128), bf16),
             dma((6,)),
-            dma((8,)),
-            dma((8,)),
+            dma((16,)),
+            dma((16,)),
             dma((32,)),
             dma((32,)),
             dma((16,)),
             dma((16,)),
             dma((16,)),
             dma((16,)),
+            pltpu.SemaphoreType.REGULAR,
         ],
         compiler_params=pltpu.CompilerParams(
             collective_id=0, has_side_effects=True, vmem_limit_bytes=60 * 1024 * 1024

time: 51.3 us -> 48.8 us (0.951)
  Pallas kernels: 48.9 us -> 46.4 us
    pallas_call x1, Pallas kernels: 48.9 us -> 46.4 us  [ping(): pl.pallas_call(ping_kernel, out_shape=jax.ShapeDtypeStruct((256, 128), f3...]
where the time goes in v5:
time: 48.8 us; the launch traced here: 48.6 us
  Pallas kernels  46.4 us (95%)
  local copies, waits for them, and re-layouts  1.57 us (3%)
  between operations  0.66 us (1%)
    pallas_call x1, Pallas kernels, ping(): pl.pallas_call(ping_kernel, out_shape=jax.ShapeDtypeStruct((256, 128), f3...  46.4 us
    unnamed x1, local copies, waits for them, and re-layouts  1.57 us

profile of v5, /device:TPU:1, one launch (start us, length us, event | category | flops | bytes accessed | tf_op | source)
XLA Modules:
  0.0 48.6 jit_solution(12002128967077646491)
XLA Ops:
  0.7 46.4 %shard_map.73 = f32[256,128]{1,0:T(8,128)} custom-call(f32[512]{0:T(512)} %constant.5.clone.powers_ref, s32[1]{0:T(128)S(6)} %copy.10.length_ref, bf16[2,1,256,256]{3,2,1,0:T(8,128)(2,1)} %spectra_hbm.1, s32[64,512]{1,0:T(8,128)} %col_lags_hbm.1, s32[32,512]{1,0:T(8,128)} %row_lags_hbm.1, bf16[2,8192]{1,0:T(2,128)(2,1)} %replica_hbm.1, ...), custom_call_target="tpu_custom_call" | custom-call | tf_op jit(solution)/shard_map/pallas_call | solution.py:482
  47.1 1.6 %copy.11 = f32[16,2,1024]{2,1,0:T(2,128)} copy(f32[16,2,1024]{2,1,0:T(2,128)} %bitcast.5) | data formatting | bytes 262144

commit v6 on v5

--- a/solution.py
+++ b/solution.py
@@ -299,7 +299,7 @@
     row_lags_hbm,
     replica_hbm,
     factors_hbm,
-    out_hbm,
+    out_ref,
     spectra,
     col_lags,
     row_lags,
@@ -460,17 +460,14 @@
     correlate(blocks, toeplitz, total)
     pack_echoes(total, work, leaving)
     exchange(frames, tm, leaving, returned, out_send, out_recv)
-    unpack_echoes(returned, work)
-
-    done = pltpu.make_async_copy(work, out_hbm, local_sem.at[5])
-    done.start()
+    unpack_echoes(returned, out_ref)
+
     for half in range(2):
         for ahead in RING8[:-1]:
             bin_copy(half, ahead, hyd).wait_send()
     drain(owners, owner, groups, arrived_groups, group_send, group_recv)
     drain(frames, tm, beams, arrived_beams, beam_send, beam_recv)
     drain(frames, tm, leaving, returned, out_send, out_recv)
-    done.wait()
 
 
 def ping(spectra, row_lags, col_lags, replica, rep_len):
@@ -481,9 +478,9 @@
     dma = pltpu.SemaphoreType.DMA
     return pl.pallas_call(
         ping_kernel,
-        out_shape=jax.ShapeDtypeStruct((256, 128), f32),
+        out_shape=pltpu.VMEM((256, 128), f32),
         in_specs=[smem, smem] + [hbm] * 5,
-        out_specs=hbm,
+        out_specs=pl.BlockSpec(memory_space=pltpu.VMEM),
         scratch_shapes=[
             pltpu.VMEM((2, 256, 256), bf16),
             pltpu.VMEM((COLS, BEAMS), i32),

time: 48.8 us -> 47.4 us (0.971)
  local copies, waits for them, and re-layouts: 1.57 us -> 0.66 us
  Pallas kernels: 46.4 us -> 45.9 us
    unnamed x1, local copies, waits for them, and re-layouts: 1.57 us -> 0.66 us
    pallas_call x1, Pallas kernels: 46.4 us -> 45.9 us  [ping(): pl.pallas_call(ping_kernel, out_shape=pltpu.VMEM((256, 128), f32), in_spe...]
where the time goes in v6:
time: 47.4 us; the launch traced here: 47.2 us
  Pallas kernels  45.9 us (97%)
  local copies, waits for them, and re-layouts  0.66 us (1%)
  between operations  0.66 us (1%)
    pallas_call x1, Pallas kernels, ping(): pl.pallas_call(ping_kernel, out_shape=pltpu.VMEM((256, 128), f32), in_spe...  45.9 us

profile of v6, /device:TPU:1, one launch (start us, length us, event | category | flops | bytes accessed | tf_op | source)
XLA Modules:
  0.0 47.2 jit_solution(1137163370171385273)
XLA Ops:
  0.7 45.9 %shard_map.73 = f32[256,128]{1,0:T(8,128)S(1)} custom-call(f32[512]{0:T(512)} %constant.5.clone.powers_ref, s32[1]{0:T(128)S(6)} %copy.11.length_ref, bf16[2,1,256,256]{3,2,1,0:T(8,128)(2,1)} %spectra_hbm.1, s32[64,512]{1,0:T(8,128)} %col_lags_hbm.1, s32[32,512]{1,0:T(8,128)} %row_lags_hbm.1, bf16[2,8192]{1,0:T(2,128)(2,1)} %replica_hbm.1, ...), custom_call_target="tpu_custom_call" | custom-call | tf_op jit(solution)/shard_map/pallas_call | solution.py:479
  46.5 0.7 %copy.10 = f32[16,2,1024]{2,1,0:T(2,128)} copy(f32[16,2,1024]{2,1,0:T(2,128)S(1)} %bitcast.5) | data formatting | bytes 262144

commit v7 on v6

--- a/solution.py
+++ b/solution.py
@@ -128,7 +128,7 @@
 
 
 def form_beams(sensors, weights, row_table, formed, half):
-    @pl.loop(0, HALF, unroll=4)
+    @pl.loop(0, HALF, unroll=8)
     def _(step):
         bin_at = half * HALF + step
         data = sensors[pl.ds(bin_at, 32, stride=32), :].astype(jnp.bfloat16)
@@ -144,7 +144,7 @@
 def pack_groups(formed, groups):
     low = lax.broadcasted_iota(jnp.int32, (8, 128), 1) < 64
 
-    @pl.loop(0, 4)
+    @pl.loop(0, 4, unroll=2)
     def _(quarter):
         turned = formed[:, pl.ds(pl.multiple_of(128 * quarter, 128), 128)].T
         for member in range(8):
@@ -227,7 +227,7 @@
 def invert(gathered, table, series):
     series[...] = jnp.zeros_like(series)
 
-    @pl.loop(0, 4)
+    @pl.loop(0, 4, unroll=2)
     def _(block):
         cols = pl.ds(pl.multiple_of(512 * block, 512), 512)
         total = jnp.dot(gathered[...], table[:, cols], preferred_element_type=jnp.float32)
@@ -253,11 +253,11 @@
     last = TAPS - 1
     total[...] = jnp.dot(lines(last), toeplitz[128 * last : 128 * TAPS, :], preferred_element_type=jnp.float32)
 
-    @pl.loop(0, last // 16)
+    @pl.loop(0, last // 32)
     def _(group):
-        tap = group * 16
-        data = jnp.concatenate([lines(tap + member) for member in range(16)], axis=1)
-        weights = toeplitz[pl.ds(pl.multiple_of(tap * 128, 16 * 128), 16 * 128), :]
+        tap = group * 32
+        data = jnp.concatenate([lines(tap + member) for member in range(32)], axis=1)
+        weights = toeplitz[pl.ds(pl.multiple_of(tap * 128, 32 * 128), 32 * 128), :]
         total[...] += jnp.dot(data, weights, preferred_element_type=jnp.float32)
 
 

time: 47.4 us -> 46.4 us (0.979)
  Pallas kernels: 45.9 us -> 44.9 us
    pallas_call x1, Pallas kernels: 45.9 us -> 44.9 us  [ping(): pl.pallas_call(ping_kernel, out_shape=pltpu.VMEM((256, 128), f32), in_spe...]
where the time goes in v7:
time: 46.4 us; the launch traced here: 46.2 us
  Pallas kernels  44.9 us (97%)
  local copies, waits for them, and re-layouts  0.66 us (1%)
  between operations  0.66 us (1%)
    pallas_call x1, Pallas kernels, ping(): pl.pallas_call(ping_kernel, out_shape=pltpu.VMEM((256, 128), f32), in_spe...  44.9 us

profile of v7, /device:TPU:1, one launch (start us, length us, event | category | flops | bytes accessed | tf_op | source)
XLA Modules:
  0.0 46.2 jit_solution(9983776410232547697)
XLA Ops:
  0.7 44.9 %shard_map.73 = f32[256,128]{1,0:T(8,128)S(1)} custom-call(f32[512]{0:T(512)} %constant.5.clone.powers_ref, s32[1]{0:T(128)S(6)} %copy.11.length_ref, bf16[2,1,256,256]{3,2,1,0:T(8,128)(2,1)} %spectra_hbm.1, s32[64,512]{1,0:T(8,128)} %col_lags_hbm.1, s32[32,512]{1,0:T(8,128)} %row_lags_hbm.1, bf16[2,8192]{1,0:T(2,128)(2,1)} %replica_hbm.1, ...), custom_call_target="tpu_custom_call" | custom-call | tf_op jit(solution)/shard_map/pallas_call | solution.py:479
  45.6 0.7 %copy.10 = f32[16,2,1024]{2,1,0:T(2,128)} copy(f32[16,2,1024]{2,1,0:T(2,128)S(1)} %bitcast.5) | data formatting | bytes 262144
